TPU v7x, 768 devices: a whole 4x8x12 slice. The times are simulated.
768 devices in a mesh: gx: 16 (over y, x_hi), gy: 4 (over x_lo, core), gz: 12 (over z).
Axes of the slice: x: 4 (x_hi: 2, x_lo: 2; x = x_hi * 2 + x_lo), y: 8, z: 12, core: 2. Of those that a mesh axis runs over, the one named last changes fastest.
Arguments:
- rhs: float32 [3, 128, 64, 1536], P(None, 'gx', 'gy', 'gz'), may hold values from -24 to 24
- conductivity: float32 [8], replicated, may hold values from 0.1 to 10
- fraction: float32 [3, 128, 64, 1536], P(None, 'gx', 'gy', 'gz'), may hold values from 0.5 to 2
- region: int32 [128, 64, 1536], P('gx', 'gy', 'gz'), may hold values from 0 to 7
- flags: int32 [3, 128, 64, 1536], P(None, 'gx', 'gy', 'gz'), may hold values 0 or 1
Outputs:
- preconditioned: float32 [3, 128, 64, 1536], P(None, 'gx', 'gy', 'gz')
All inputs are finite; a program needn't handle non-finite values. No bound on the sum of `flags` on one device may be relied on, other than what follows from the above.
Results may differ from a plain program's by a relative error of at most 0.00002.
Values sent between devices are 32-bit elements; how exact they have to be, the bound alone decides.
No kernel may reach another device: no remote copies, remote signals or barrier semaphores. Data moves between devices by JAX's collectives and lax.ppermute only.
A program may use at most 32 MiB of HBM per device.

v0:
```python
import jax
import jax.numpy as jnp
from jax import lax
from jax.sharding import PartitionSpec as P

edge_damping = 0.8
node_damping = 0.8


def with_halo(cells, sides, width):
    for axis, dim in sides:
        count = lax.axis_size(axis)
        head = lax.slice_in_dim(cells, 0, width, axis=dim)
        tail = lax.slice_in_dim(cells, cells.shape[dim] - width, cells.shape[dim], axis=dim)
        cells = jnp.concatenate(
            [
                lax.ppermute(tail, axis, [(i, (i + 1) % count) for i in range(count)]),
                cells,
                lax.ppermute(head, axis, [((i + 1) % count, i) for i in range(count)]),
            ],
            axis=dim,
        )
    return cells


def upward(field, spatial):
    return jnp.roll(field, -1, axis=spatial)


def downward(field, spatial):
    return jnp.roll(field, 1, axis=spatial)


def forward_diff(field, spatial):
    return upward(field, spatial) - field


def backward_adjoint(field, spatial):
    return downward(field, spatial) - field


def curl_curl(stacked):
    first, second, third = (stacked[0], stacked[1], stacked[2])
    face_zero = forward_diff(third, 1) - forward_diff(second, 2)
    face_one = forward_diff(first, 2) - forward_diff(third, 0)
    face_two = forward_diff(second, 0) - forward_diff(first, 1)
    return jnp.stack(
        [
            backward_adjoint(face_one, 2) - backward_adjoint(face_two, 1),
            backward_adjoint(face_two, 0) - backward_adjoint(face_zero, 2),
            backward_adjoint(face_zero, 1) - backward_adjoint(face_one, 0),
        ]
    )


def conductance(conductivity, region):
    total = jnp.zeros(region.shape, conductivity.dtype)
    for number in range(conductivity.shape[0]):
        total = total + jnp.where(
            region == number, conductivity[number], jnp.zeros((), conductivity.dtype)
        )
    return total


def crop(array, width):
    leading = (slice(None),) * (array.ndim - 3)
    return array[leading + (slice(width, -width),) * 3]


def nodal_operator(stacked):
    result = 7.0 * stacked
    for spatial in range(3):
        result = result - (
            jnp.roll(stacked, -1, axis=spatial + 1) + jnp.roll(stacked, 1, axis=spatial + 1)
        )
    return result


def nodal_part(masked_res):
    gradient_rhs = backward_adjoint(masked_res[0], 0)
    for spatial in range(1, 3):
        gradient_rhs = gradient_rhs + backward_adjoint(masked_res[spatial], spatial)
    vector_rhs = [
        (masked_res[spatial] + downward(masked_res[spatial], spatial)) * 0.5 for spatial in range(3)
    ]
    nodal_rhs = jnp.stack([gradient_rhs] + vector_rhs)
    first_node = node_damping * nodal_rhs / 7.0
    second_node = first_node + node_damping * (nodal_rhs - nodal_operator(first_node)) / 7.0
    potential = second_node[0]
    parts = [
        forward_diff(potential, spatial)
        + (second_node[spatial + 1] + upward(second_node[spatial + 1], spatial)) * 0.5
        for spatial in range(3)
    ]
    return jnp.stack(parts)


def operator_shrunk(field, keeping, sigma):
    masked = keeping * field
    return crop(keeping * (curl_curl(masked) + sigma * masked) + (1.0 - keeping) * field, 1)


def unpack_wide(wide):
    wide_rhs = wide[0:3]
    wide_sigma = wide[3:6]
    wide_keep = (wide_sigma > 0.0).astype(wide_sigma.dtype)
    return (wide_rhs, wide_sigma, wide_keep)


def on_device(rhs, conductivity, fraction, region, flags):
    sigma = conductance(conductivity, region)[None] * fraction
    keeping = 1.0 - flags.astype(jnp.float32)
    packed = jnp.concatenate([rhs, keeping * sigma], axis=0)
    wide = with_halo(packed, (("gx", 1), ("gy", 2), ("gz", 3)), 4)
    wide_rhs, wide_sigma, wide_keep = unpack_wide(wide)
    wide_inverse = 1.0 / (wide_keep * (4.0 + wide_sigma) + (1.0 - wide_keep))
    first_iter = edge_damping * wide_inverse * wide_rhs
    applied = operator_shrunk(first_iter, wide_keep, wide_sigma)
    second_wide = crop(first_iter, 1) + edge_damping * crop(wide_inverse, 1) * (
        crop(wide_rhs, 1) - applied
    )
    inner_keep = crop(wide_keep, 2)
    residual_wide = crop(wide_rhs, 2) - operator_shrunk(
        second_wide, crop(wide_keep, 1), crop(wide_sigma, 1)
    )
    second_iter = crop(second_wide, 3)
    correction = keeping * crop(nodal_part(inner_keep * residual_wide), 2)
    return second_iter + correction


def solution(mesh):
    return jax.shard_map(
        on_device,
        mesh=mesh,
        in_specs=(
            P(None, "gx", "gy", "gz"),
            P(),
            P(None, "gx", "gy", "gz"),
            P("gx", "gy", "gz"),
            P(None, "gx", "gy", "gz"),
        ),
        out_specs=P(None, "gx", "gy", "gz"),
        check_vma=False,
    )
```

profile of v0, /device:TPU:1, one launch (start us, length us, event | category | flops | bytes accessed | tf_op | source)
XLA Modules:
  0.0 79.2 jit_solution(10471694943243369783)
XLA Ops:
  0.0 1.6 %fusion.66 = (f32[1]{0:T(128)}, f32[1]{0:T(128)}, f32[1]{0:T(128)}, f32[1]{0:T(128)}, f32[1]{0:T(128)}, /*index=5*/f32[1]{0:T(128)}, f32[1]{0:T(128)}, f32[1]{0:T(128)}) fusion(f32[8]{0:T(128)} %param.6), kind=kLoop, calls=%fused_computation.212 | loop fusion | bytes 64 | tf_op jit(solution)/shard_map/slice | solution.py:60
  1.6 5.9 %select_add_fusion = f32[8,16,128]{2,1,0:T(8,128)S(1)} fusion(s32[8,16,128]{2,1,0:T(8,128)} %param.8, f32[]{:T(128)} %bitcast.7, f32[]{:T(128)} %bitcast.6, f32[]{:T(128)} %bitcast.5, f32[]{:T(128)} %bitcast.4, f32[]{:T(128)} %bitcast.3, f32[]{:T(128)} %bitcast.2, f32[]{:T(128)} %bitcast.1, f32[]{:T(128)} %bitcast), kind=kLoop, calls=%fused_computation.161 | loop fusion | flops 376832 | bytes 131104 | tf_op jit(solution)/shard_map/add | solution.py:59
  7.5 1.1 %multiply_multiply_fusion = f32[3,8,16,128]{3,2,1,0:T(8,128)S(1)} fusion(f32[3,8,16,128]{3,2,1,0:T(8,128)} %param.7, s32[3,8,16,128]{3,2,1,0:T(8,128)} %param.9, f32[8,16,128]{2,1,0:T(8,128)S(1)} %select_add_fusion), kind=kLoop, calls=%fused_computation.154 | loop fusion | flops 196608 | bytes 655360 | tf_op jit(solution)/shard_map/mul | solution.py:113
  8.6 1.0 %fusion.42 = (f32[6,4,16,128]{3,2,1,0:T(8,128)S(1)}, f32[6,4,16,128]{3,2,1,0:T(8,128)S(1)}) fusion(f32[3,8,16,128]{3,2,1,0:T(8,128)} %param.5, f32[3,8,16,128]{3,2,1,0:T(8,128)S(1)} %multiply_multiply_fusion), kind=kLoop, calls=%fused_computation.142 | loop fusion | flops 98304 | bytes 786432 | tf_op jit(solution)/shard_map/concatenate | solution.py:113
  9.6 5.5 %collective-permute-start = (f32[6,4,16,128]{3,2,1,0:T(8,128)S(1)}, f32[6,4,16,128]{3,2,1,0:T(8,128)S(1)}, u32[]{:S(2)}, u32[]{:S(2)}) collective-permute-start(f32[6,4,16,128]{3,2,1,0:T(8,128)S(1)} %get-tuple-element.101), channel_id=1, source_target_pairs={{0,48},{48,96},{96,144},{144,192},{192,240},{240,288},{288,336},{3... | collective-permute-start | bytes 589832 | tf_op jit(solution)/shard_map/ppermute | solution.py:17
  15.1 4.8 %collective-permute-start.1 = (f32[6,4,16,128]{3,2,1,0:T(8,128)S(1)}, f32[6,4,16,128]{3,2,1,0:T(8,128)S(1)}, u32[]{:S(2)}, u32[]{:S(2)}) collective-permute-start(f32[6,4,16,128]{3,2,1,0:T(8,128)S(1)} %get-tuple-element.102), channel_id=1, source_target_pairs={{48,0},{96,48},{144,96},{192,144},{240,192},{288,240},{336,288},{3... | collective-permute-start | bytes 589832 | tf_op jit(solution)/shard_map/ppermute | solution.py:19
  19.9 1.1 %collective-permute-done = f32[6,4,16,128]{3,2,1,0:T(8,128)S(1)} collective-permute-done((f32[6,4,16,128]{3,2,1,0:T(8,128)S(1)}, f32[6,4,16,128]{3,2,1,0:T(8,128)S(1)}, u32[]{:S(2)}, u32[]{:S(2)}) %collective-permute-start) | collective-permute-done | bytes 196640 | tf_op jit(solution)/shard_map/ppermute | solution.py:17
  21.0 2.1 %collective-permute-done.1 = f32[6,4,16,128]{3,2,1,0:T(8,128)S(1)} collective-permute-done((f32[6,4,16,128]{3,2,1,0:T(8,128)S(1)}, f32[6,4,16,128]{3,2,1,0:T(8,128)S(1)}, u32[]{:S(2)}, u32[]{:S(2)}) %collective-permute-start.1) | collective-permute-done | bytes 196640 | tf_op jit(solution)/shard_map/ppermute | solution.py:19
  23.2 7.3 %collective-permute-start.2 = (f32[6,16,4,128]{3,2,1,0:T(4,128)S(1)}, f32[6,16,4,128]{3,2,1,0:T(4,128)S(1)}, u32[]{:S(2)}, u32[]{:S(2)}) collective-permute-start(f32[6,16,4,128]{3,2,1,0:T(4,128)S(1)} %get-tuple-element.83), channel_id=1, source_target_pairs={{0,12},{12,24},{24,36},{36,0},{1,13},{13,25},{25,37},{37,1},{2,14}... | collective-permute-start | bytes 589832 | tf_op jit(solution)/shard_map/ppermute | solution.py:17
  30.5 6.5 %collective-permute-start.3 = (f32[6,16,4,128]{3,2,1,0:T(4,128)S(1)}, f32[6,16,4,128]{3,2,1,0:T(4,128)S(1)}, u32[]{:S(2)}, u32[]{:S(2)}) collective-permute-start(f32[6,16,4,128]{3,2,1,0:T(4,128)S(1)} %get-tuple-element.84), channel_id=1, source_target_pairs={{12,0},{24,12},{36,24},{0,36},{13,1},{25,13},{37,25},{1,37},{14,2}... | collective-permute-start | bytes 589832 | tf_op jit(solution)/shard_map/ppermute | solution.py:19
  37.1 1.0 %collective-permute-done.3 = f32[6,16,4,128]{3,2,1,0:T(4,128)S(1)} collective-permute-done((f32[6,16,4,128]{3,2,1,0:T(4,128)S(1)}, f32[6,16,4,128]{3,2,1,0:T(4,128)S(1)}, u32[]{:S(2)}, u32[]{:S(2)}) %collective-permute-start.3) | collective-permute-done | bytes 196640 | tf_op jit(solution)/shard_map/ppermute | solution.py:19
  38.1 0.2 pad_maximum_fusion.1
  38.3 0.4 fusion.63
  38.7 1.4 %copy.96 = f32[6,16,24,4]{2,1,3,0:T(8,128)} copy(f32[6,16,24,4]{3,2,1,0:T(8,128)S(1)} %get-tuple-element.65) | data formatting | bytes 73728 | tf_op jit(solution)/shard_map/slice | solution.py:14
  40.1 3.4 %collective-permute-start.4 = (f32[6,16,24,4]{2,1,3,0:T(8,128)}, f32[6,16,24,4]{2,1,3,0:T(8,128)S(1)}, u32[]{:S(2)}, u32[]{:S(2)}) collective-permute-start(f32[6,16,24,4]{2,1,3,0:T(8,128)} %copy.96), channel_id=1, source_target_pairs={{0,1},{1,2},{2,3},{3,4},{4,5},{5,6},{6,7},{7,8},{8,9},{9,10},{10,1... | collective-permute-start | bytes 110600 | tf_op jit(solution)/shard_map/ppermute | solution.py:17
  43.5 0.7 copy.97
  44.1 12.2 %collective-permute-start.5 = (f32[6,16,24,4]{2,1,3,0:T(8,128)S(1)}, f32[6,16,24,4]{2,1,3,0:T(8,128)}, u32[]{:S(2)}, u32[]{:S(2)}) collective-permute-start(f32[6,16,24,4]{2,1,3,0:T(8,128)S(1)} %copy.97), channel_id=1, source_target_pairs={{1,0},{2,1},{3,2},{4,3},{5,4},{6,5},{7,6},{8,7},{9,8},{10,9},{11,1... | collective-permute-start | bytes 110600 | tf_op jit(solution)/shard_map/ppermute | solution.py:19
  56.4 2.2 %collective-permute-done.4 = f32[6,16,24,4]{2,1,3,0:T(8,128)S(1)} collective-permute-done((f32[6,16,24,4]{2,1,3,0:T(8,128)}, f32[6,16,24,4]{2,1,3,0:T(8,128)S(1)}, u32[]{:S(2)}, u32[]{:S(2)}) %collective-permute-start.4) | collective-permute-done | bytes 36896 | tf_op jit(solution)/shard_map/ppermute | solution.py:17
  58.6 0.6 copy.98
  59.3 1.6 %collective-permute-done.5 = f32[6,16,24,4]{2,1,3,0:T(8,128)} collective-permute-done((f32[6,16,24,4]{2,1,3,0:T(8,128)S(1)}, f32[6,16,24,4]{2,1,3,0:T(8,128)}, u32[]{:S(2)}, u32[]{:S(2)}) %collective-permute-start.5) | collective-permute-done | bytes 36896 | tf_op jit(solution)/shard_map/ppermute | solution.py:19
  60.9 1.6 %copy.99 = f32[6,16,24,4]{3,2,1,0:T(8,128)S(1)} copy(f32[6,16,24,4]{2,1,3,0:T(8,128)} %collective-permute-done.5) | data formatting | bytes 73728 | tf_op jit(solution)/shard_map/ppermute | solution.py:19
  62.4 1.4 %pad_maximum_fusion = f32[6,16,24,136]{3,2,1,0:T(8,128)S(1)} fusion(f32[6,16,24,4]{3,2,1,0:T(8,128)S(1)} %copy.99, f32[6,16,4,128]{3,2,1,0:T(4,128)S(1)} %collective-permute-done.3, f32[6,4,16,128]{3,2,1,0:T(8,128)S(1)} %collective-permute-done.1, f32[3,8,16,128]{3,2,1,0:T(8,128)S(1)} %multiply_multiply_fusion, f32[3,8,16,128]{3,2,1,0:T(8,128)S(1)} %copy-done, ...), kind=kLoop, calls=%fused_computation | loop fusion | flops 2193408 | bytes 2506752 | tf_op jit(solution)/shard_map/concatenate | solution.py:15
  63.9 0.2 fusion.49
  64.1 0.6 broadcast_select_fusion
  64.8 0.3 slice_bitcast_fusion.67
  65.4 0.4 fusion.24
  66.3 0.3 fusion.19
  66.6 0.3 fusion.23
  66.9 0.1 fusion.26
  67.1 2.7 %slice_multiply_fusion.6 = (f32[3,14,22,134]{3,2,1,0:T(8,128)S(1)}, f32[3,14,22,134]{3,2,1,0:T(8,128)S(1)}, f32[3,14,22,134]{3,2,1,0:T(8,128)S(1)}, f32[3,14,22,134]{3,2,1,0:T(8,128)S(1)}) fusion(f32[3,16,24,136]{3,2,1,0:T(8,128)S(1)} %get-tuple-element.12, f32[3,16,24,136]{3,2,1,0:T(8,128)S(1)} %get-tuple-element.119, ...), kind=kLoop, calls=%fused_computation.197 | loop fusion | flops 1485792 | bytes 6693672 | tf_op jit(solution)/shard_map/mul | solution.py:99
  70.0 0.2 slice_bitcast_fusion.61
  70.3 0.2 slice_bitcast_fusion.64
  70.5 0.4 fusion.33
  71.4 0.3 fusion.28
  71.7 0.3 fusion.32
  72.1 1.7 %fusion.14 = f32[3,12,20,132]{3,2,1,0:T(8,128)S(1)} fusion(f32[3,14,22,134]{3,2,1,0:T(8,128)S(1)} %get-tuple-element.11, f32[1,14,22,134]{3,2,1,0:T(8,128)S(1)} %fusion.35, f32[3,14,22,134]{3,2,1,0:T(8,128)S(1)} %get-tuple-element.10, f32[3,14,22,134]{3,2,1,0:T(8,128)S(1)} %get-tuple-element.22, f32[1,14,22,134]{3,2,1,0:T(8,128)S(1)} %get-tuple-element.8, ...), kind=kLoop, calls=%fused_computation.28 | loop fusion | flops 950400 | bytes 3156384 | tf_op jit(solution)/shard_map/mul | solution.py:127
  74.1 0.2 subtract_add_fusion
  74.3 0.1 fusion.17
  74.6 0.4 fusion.55
  75.0 0.2 fusion.60
  75.1 0.4 fusion.56
  75.5 0.2 fusion.58
  75.7 1.1 %fusion.5 = f32[4,12,20,132]{3,2,1,0:T(8,128)S(1)} fusion(f32[4,1,20,132]{3,2,1,0:T(8,128)S(1)} %get-tuple-element.47, f32[4,11,20,132]{3,2,1,0:T(8,128)S(1)} %get-tuple-element.49, f32[4,11,20,132]{3,2,1,0:T(8,128)S(1)} %get-tuple-element.48, f32[4,1,20,132]{3,2,1,0:T(8,128)S(1)} %get-tuple-element.46, f32[4,12,1,132]{3,2,1,0:T(1,128)S(1)} %get-tuple-element.43, ...), kind=kLoop, calls=%fused_computation.10 | loop fusion | flops 2534400 | bytes 4055040 | tf_op jit(solution)/shard_map/add | solution.py:88
  77.0 0.1 slice_bitcast_fusion.18
  77.2 0.1 slice_bitcast_fusion.19
  77.4 0.3 fusion.37
  77.7 0.6 copy-done.1
  78.3 0.9 %fusion.44 = f32[3,8,16,128]{3,2,1,0:T(8,128)} fusion(f32[1,12,20,132]{3,2,1,0:T(8,128)S(1)} %get-tuple-element.30, f32[1,12,20,132]{3,2,1,0:T(8,128)S(1)} %get-tuple-element.29, f32[1,12,20,132]{3,2,1,0:T(8,128)S(1)} %get-tuple-element.28, f32[3,14,22,134]{3,2,1,0:T(8,128)S(1)} %get-tuple-element.11, s32[3,8,16,128]{3,2,1,0:T(8,128)S(1)} %copy-done.1), kind=kLoop, calls=%fused_computation.145 | loop fusion | flops 294912 | bytes 969984 | tf_op jit(solution)/shard_map/add | solution.py:128
  (63 shorter events, 2.2 us)
Async XLA Ops:
  0.0 23.1 %copy-start = (f32[3,8,16,128]{3,2,1,0:T(8,128)S(1)}, f32[3,8,16,128]{3,2,1,0:T(8,128)}, u32[]{:S(2)}) copy-start(f32[3,8,16,128]{3,2,1,0:T(8,128)} %param.5) | copy-start | bytes 589828
  9.6 11.4 %collective-permute-start = (f32[6,4,16,128]{3,2,1,0:T(8,128)S(1)}, f32[6,4,16,128]{3,2,1,0:T(8,128)S(1)}, u32[]{:S(2)}, u32[]{:S(2)}) collective-permute-start(f32[6,4,16,128]{3,2,1,0:T(8,128)S(1)} %get-tuple-element.101), channel_id=1, source_target_pairs={{0,48},{48,96},{96,144},{144,192},{192,240},{240,288},{288,336},{3... | collective-permute-start | bytes 589832 | tf_op jit(solution)/shard_map/ppermute | solution.py:17
  15.1 8.1 %collective-permute-start.1 = (f32[6,4,16,128]{3,2,1,0:T(8,128)S(1)}, f32[6,4,16,128]{3,2,1,0:T(8,128)S(1)}, u32[]{:S(2)}, u32[]{:S(2)}) collective-permute-start(f32[6,4,16,128]{3,2,1,0:T(8,128)S(1)} %get-tuple-element.102), channel_id=1, source_target_pairs={{48,0},{96,48},{144,96},{192,144},{240,192},{288,240},{336,288},{3... | collective-permute-start | bytes 589832 | tf_op jit(solution)/shard_map/ppermute | solution.py:19
  23.2 13.9 %collective-permute-start.2 = (f32[6,16,4,128]{3,2,1,0:T(4,128)S(1)}, f32[6,16,4,128]{3,2,1,0:T(4,128)S(1)}, u32[]{:S(2)}, u32[]{:S(2)}) collective-permute-start(f32[6,16,4,128]{3,2,1,0:T(4,128)S(1)} %get-tuple-element.83), channel_id=1, source_target_pairs={{0,12},{12,24},{24,36},{36,0},{1,13},{13,25},{25,37},{37,1},{2,14}... | collective-permute-start | bytes 589832 | tf_op jit(solution)/shard_map/ppermute | solution.py:17
  30.5 7.6 %collective-permute-start.3 = (f32[6,16,4,128]{3,2,1,0:T(4,128)S(1)}, f32[6,16,4,128]{3,2,1,0:T(4,128)S(1)}, u32[]{:S(2)}, u32[]{:S(2)}) collective-permute-start(f32[6,16,4,128]{3,2,1,0:T(4,128)S(1)} %get-tuple-element.84), channel_id=1, source_target_pairs={{12,0},{24,12},{36,24},{0,36},{13,1},{25,13},{37,25},{1,37},{14,2}... | collective-permute-start | bytes 589832 | tf_op jit(solution)/shard_map/ppermute | solution.py:19
  40.1 18.6 %collective-permute-start.4 = (f32[6,16,24,4]{2,1,3,0:T(8,128)}, f32[6,16,24,4]{2,1,3,0:T(8,128)S(1)}, u32[]{:S(2)}, u32[]{:S(2)}) collective-permute-start(f32[6,16,24,4]{2,1,3,0:T(8,128)} %copy.96), channel_id=1, source_target_pairs={{0,1},{1,2},{2,3},{3,4},{4,5},{5,6},{6,7},{7,8},{8,9},{9,10},{10,1... | collective-permute-start | bytes 110600 | tf_op jit(solution)/shard_map/ppermute | solution.py:17
  44.1 16.7 %collective-permute-start.5 = (f32[6,16,24,4]{2,1,3,0:T(8,128)S(1)}, f32[6,16,24,4]{2,1,3,0:T(8,128)}, u32[]{:S(2)}, u32[]{:S(2)}) collective-permute-start(f32[6,16,24,4]{2,1,3,0:T(8,128)S(1)} %copy.97), channel_id=1, source_target_pairs={{1,0},{2,1},{3,2},{4,3},{5,4},{6,5},{7,6},{8,7},{9,8},{10,9},{11,1... | collective-permute-start | bytes 110600 | tf_op jit(solution)/shard_map/ppermute | solution.py:19
  77.4 0.9 %copy-start.1 = (s32[3,8,16,128]{3,2,1,0:T(8,128)S(1)}, s32[3,8,16,128]{3,2,1,0:T(8,128)}, u32[]{:S(2)}) copy-start(s32[3,8,16,128]{3,2,1,0:T(8,128)} %param.9) | copy-start | bytes 589828
where the time goes:
time: 79.7 us; the launch traced here: 79.2 us
  starting transfers between devices  39.8 us (50%)
  other arithmetic  19.7 us (25%)
  local copies, waits for them, and re-layouts  10.9 us (14%)
  waiting for transfers between devices  8.11 us (10%)
    ppermute x3, starting transfers between devices, with_halo(): lax.ppermute(head, axis, [((i + 1) % count, i) for i in range(count)])  23.6 us
    ppermute x3, starting transfers between devices, with_halo(): lax.ppermute(tail, axis, [(i, (i + 1) % count) for i in range(count)])  16.2 us
    add x1, other arithmetic, conductance(): total + jnp.where(region == number, conductivity[number], jnp.zeros((), c...  5.92 us
    ppermute x3, waiting for transfers between devices, with_halo(): lax.ppermute(head, axis, [((i + 1) % count, i) for i in range(count)])  4.73 us
    ppermute x3, waiting for transfers between devices, with_halo(): lax.ppermute(tail, axis, [(i, (i + 1) % count) for i in range(count)])  3.38 us
    mul x2, other arithmetic, operator_shrunk(): masked = keeping * field  3.3 us
    slice x2, local copies, waits for them, and re-layouts, with_halo(): lax.slice_in_dim(cells, cells.shape[dim] - width, cells.shape[dim], axis=...  1.75 us
    mul x1, other arithmetic, on_device(): correction = keeping * crop(nodal_part(inner_keep * residual_wide), 2)  1.73 us
  transfers between devices with their start and end apart: 6, of which 5 were waited for; matrix products, arithmetic and copies ran while one was open for 2% of the time, Pallas kernels for 0%

commit v1 on v0

v1 whole, which is shorter than its diff:
```python
import functools

import jax
import jax.numpy as jnp
from jax import lax
from jax.experimental import pallas as pl
from jax.experimental.pallas import tpu as pltpu
from jax.sharding import PartitionSpec as P

EDGE = 0.8
NODE = 0.8 / 7.0

BX, BY, BZ = 8, 16, 128
LOW, HIGH = 3, 4
EXT = LOW + BX + HIGH
ROWS = 6 * BY + 8
YMAIN = EXT * 24
YROWS = YMAIN + 64
VMEM_LIMIT = 16 * 1024 * 1024

VMEM = pl.BlockSpec(memory_space=pltpu.VMEM)
SMEM = pl.BlockSpec(memory_space=pltpu.SMEM)


def call(body, out_shape, n_vmem, n_smem, name, scratch=(), flops=1000000):
    return pl.pallas_call(
        body,
        out_shape=out_shape,
        in_specs=[SMEM] * n_smem + [VMEM] * n_vmem,
        out_specs=jax.tree.map(lambda _: VMEM, out_shape),
        scratch_shapes=list(scratch),
        compiler_params=pltpu.CompilerParams(vmem_limit_bytes=VMEM_LIMIT),
        cost_estimate=pl.CostEstimate(flops=flops, bytes_accessed=1000000, transcendentals=0),
        name=name,
    )


def lanes(shape):
    return lax.broadcasted_iota(jnp.int32, shape, 1)


def rotate(v, shift, axis):
    return pltpu.roll(v, shift % v.shape[axis], axis)


def prepare(cond, rhs, fraction, region, flags, sigma_out, packed_out):
    group = lanes((8, BZ)) // 8
    for x in range(BX):
        where = region[x]
        conductivity = jnp.full((BY, BZ), cond[0], jnp.float32)
        for number in range(1, 8):
            conductivity = jnp.where(where == number, cond[number], conductivity)
        packed = jnp.zeros((8, BZ), jnp.float32)
        for field in range(6):
            if field < 3:
                value = rhs[field, x]
            else:
                value = jnp.where(flags[field - 3, x] == 0, conductivity * fraction[field - 3, x], 0.0)
                sigma_out[field - 3, x] = value
            for tile in range(2):
                slot = field * 2 + tile
                moved = rotate(value[tile * 8 : tile * 8 + 8], LOW + 8 * slot, 1)
                packed = jnp.where(group == slot, moved, packed)
        packed_out[x] = packed


def send_x(zpar, rhs, sigma, first, second, up_out, down_out, packed_out):
    even = zpar[0] == 0
    below = (lanes((8, BZ)) % 8) < LOW
    for x in range(BX):
        from_high = jnp.where(even, first[1, x], second[1, x])
        from_low = jnp.where(even, second[0, x], first[0, x])
        packed = jnp.where(below, from_low, from_high)
        packed_out[x] = packed
        for out, plane in ((up_out, x - (BX - LOW)), (down_out, x)):
            if not 0 <= plane < out.shape[0]:
                continue
            for c in range(3):
                out[plane, c * BY : (c + 1) * BY] = rhs[c, x]
                out[plane, (3 + c) * BY : (4 + c) * BY] = sigma[c, x]
            out[plane, 6 * BY :] = packed


def plane_rows(p, field, rows, rhs, sigma, low, high):
    if p < LOW:
        return low[p, field * BY + rows.start : field * BY + rows.stop]
    if p >= LOW + BX:
        return high[p - LOW - BX, field * BY + rows.start : field * BY + rows.stop]
    return (rhs if field < 3 else sigma)[field % 3, p - LOW, rows]


def plane_packed(p, rows, packed, low, high):
    if p < LOW:
        return low[p, 6 * BY + rows.start : 6 * BY + rows.stop]
    if p >= LOW + BX:
        return high[p - LOW - BX, 6 * BY + rows.start : 6 * BY + rows.stop]
    return packed[p - LOW, rows]


def send_y(ypar, rhs, sigma, packed, low, high, first_out, second_out):
    def fill(top_out, bottom_out):
        for p in range(EXT):
            for out, rows, prow in ((top_out, slice(BY - 4, BY), slice(4, 8)), (bottom_out, slice(0, 4), slice(0, 4))):
                for field in range(6):
                    at = p * 24 + field * 4
                    out[at : at + 4] = plane_rows(p, field, rows, rhs, sigma, low, high)
                at = YMAIN + p * 4
                out[at : at + 4] = plane_packed(p, prow, packed, low, high)

    for out in (first_out, second_out):
        out[YMAIN + EXT * 4 :] = jnp.zeros((YROWS - YMAIN - EXT * 4, BZ), jnp.float32)

    @pl.when(ypar[0] == 0)
    def _():
        fill(first_out, second_out)

    @pl.when(ypar[0] != 0)
    def _():
        fill(second_out, first_out)


def up_y(v):
    return rotate(v, -1, 0)


def down_y(v):
    return rotate(v, 1, 0)


def up_z(v):
    return rotate(v, -1, 1)


def down_z(v):
    return rotate(v, 1, 1)


def stencil(ypar, rhs, sigma, packed, low, high, first, second, out, wide, weight, iterate, second_iter, nodal):
    even = ypar[0] == 0
    upper = lax.broadcasted_iota(jnp.int32, (8, BZ), 0) < 4

    for p in range(EXT):
        halves = []
        at = YMAIN + p * 4
        above = jnp.where(even, first[1, at : at + 4], second[1, at : at + 4])
        below = jnp.where(even, second[0, at : at + 4], first[0, at : at + 4])
        edge = jnp.concatenate([above, below], axis=0)
        edge = jnp.where(upper, edge, rotate(edge, -8, 1))
        whole = plane_packed(p, slice(0, 8), packed, low, high)
        for field in range(6):
            at = p * 24 + field * 4
            above = jnp.where(even, first[1, at : at + 4], second[1, at : at + 4])
            below = jnp.where(even, second[0, at : at + 4], first[0, at : at + 4])
            wide[field, p, 0:BY, 0:BZ] = plane_rows(p, field, slice(0, BY), rhs, sigma, low, high)
            wide[field, p, BY:24, 0:BZ] = jnp.concatenate([above, below], axis=0)
            wide[field, p, 0:8, BZ:] = rotate(whole, -(LOW + 16 * field), 1)
            wide[field, p, 8:16, BZ:] = rotate(whole, -(LOW + 16 * field + 8), 1)
            wide[field, p, 16:24, BZ:] = rotate(edge, -(LOW + 16 * field), 1)
        for c in range(3):
            s = wide[3 + c, p]
            w = jnp.where(s > 0.0, EDGE / (4.0 + s), 0.0)
            weight[c, p] = w
            iterate[c, p] = w * wide[c, p]

    def faces(u, p):
        u0, u1, u2 = u[0, p], u[1, p], u[2, p]
        f0 = (up_y(u2) - u2) - (up_z(u1) - u1)
        f1 = (up_z(u0) - u0) - (u[2, p + 1] - u2)
        f2 = (u[1, p + 1] - u1) - (up_y(u0) - u0)
        return f0, f1, f2

    def curl0(f):
        return (down_z(f[1]) - f[1]) - (down_y(f[2]) - f[2])

    def curl1(f, prev):
        return (prev[2] - f[2]) - (down_z(f[0]) - f[0])

    def curl2(f, prev):
        return (down_y(f[0]) - f[0]) - (prev[1] - f[1])

    prev = faces(iterate, 0)
    for p in range(1, EXT - 1):
        f = faces(iterate, p)
        for c, k in enumerate((curl0(f), curl1(f, prev), curl2(f, prev))):
            u = iterate[c, p]
            second_iter[c, p] = u + weight[c, p] * (wide[c, p] - (k + wide[3 + c, p] * u))
        prev = f

    def residual(c, p, k):
        s = wide[3 + c, p]
        return jnp.where(s > 0.0, wide[c, p] - (k + s * second_iter[c, p]), 0.0)

    prev = faces(second_iter, 1)
    before = residual(0, 1, curl0(prev))
    for p in range(2, EXT - 2):
        f = faces(second_iter, p)
        q0 = residual(0, p, curl0(f))
        q1 = residual(1, p, curl1(f, prev))
        q2 = residual(2, p, curl2(f, prev))
        d1, d2 = down_y(q1), down_z(q2)
        nodal[0, p] = (before - q0) + (d1 - q1) + (d2 - q2)
        nodal[1, p] = (before + q0) * 0.5
        nodal[2, p] = (d1 + q1) * 0.5
        nodal[3, p] = (d2 + q2) * 0.5
        prev, before = f, q0

    def node(c, p):
        b = nodal[c, p]
        near = (nodal[c, p - 1] + nodal[c, p + 1]) + (up_y(b) + down_y(b)) + (up_z(b) + down_z(b))
        return (1.2 * NODE) * b + (NODE * NODE) * near

    n0, n1 = node(0, LOW), node(1, LOW)
    for x in range(BX):
        p = x + LOW
        n0_next, n1_next = node(0, p + 1), node(1, p + 1)
        n2, n3 = node(2, p), node(3, p)
        corrections = (
            (n0_next - n0) + (n1_next + n1) * 0.5,
            (up_y(n0) - n0) + (n2 + up_y(n2)) * 0.5,
            (up_z(n0) - n0) + (n3 + up_z(n3)) * 0.5,
        )
        for c in range(3):
            kept = second_iter[c, p, 0:BY, 0:BZ] + corrections[c][0:BY, 0:BZ]
            out[c, x] = jnp.where(sigma[c, x] > 0.0, kept, 0.96 * rhs[c, x])
        n0, n1 = n0_next, n1_next


def pairs(count):
    return (
        [[i, i + 1] for i in range(0, count, 2)],
        [[i, (i + 1) % count] for i in range(1, count, 2)],
    )


def gather(value, axis, groups):
    return lax.all_gather(value, axis, axis=0, tiled=False, axis_index_groups=groups)


def on_device(rhs, conductivity, fraction, region, flags):
    f32 = functools.partial(jax.ShapeDtypeStruct, dtype=jnp.float32)
    parity = lambda axis: (lax.axis_index(axis) % 2).astype(jnp.int32).reshape(1)
    ypar, zpar = parity("gy"), parity("gz")

    sigma, packed = call(prepare, (f32((3, BX, BY, BZ)), f32((BX, 8, BZ))), 4, 1, "prepare")(
        conductivity, rhs, fraction, region, flags
    )
    even_z, odd_z = pairs(lax.axis_size("gz"))
    first = gather(packed, "gz", even_z)
    second = gather(packed, "gz", odd_z)

    up, down, packed = call(
        send_x, (f32((LOW, ROWS, BZ)), f32((HIGH, ROWS, BZ)), f32((BX, 8, BZ))), 4, 1, "send_x"
    )(zpar, rhs, sigma, first, second)
    count = lax.axis_size("gx")
    low = lax.ppermute(up, "gx", [(i, (i + 1) % count) for i in range(count)])
    high = lax.ppermute(down, "gx", [((i + 1) % count, i) for i in range(count)])

    even_y, odd_y = pairs(lax.axis_size("gy"))
    to_first, to_second = call(send_y, (f32((YROWS, BZ)), f32((YROWS, BZ))), 5, 1, "send_y")(
        ypar, rhs, sigma, packed, low, high
    )
    first = gather(to_first, "gy", even_y)
    second = gather(to_second, "gy", odd_y)

    wide = (EXT, 24, 2 * BZ)
    return call(
        stencil,
        f32((3, BX, BY, BZ)),
        7,
        1,
        "stencil",
        scratch=(
            pltpu.VMEM((6, *wide), jnp.float32),
            pltpu.VMEM((3, *wide), jnp.float32),
            pltpu.VMEM((3, *wide), jnp.float32),
            pltpu.VMEM((3, *wide), jnp.float32),
            pltpu.VMEM((4, *wide), jnp.float32),
        ),
    )(ypar, rhs, sigma, packed, low, high, first, second)


def solution(mesh):
    return jax.shard_map(
        on_device,
        mesh=mesh,
        in_specs=(
            P(None, "gx", "gy", "gz"),
            P(),
            P(None, "gx", "gy", "gz"),
            P("gx", "gy", "gz"),
            P(None, "gx", "gy", "gz"),
        ),
        out_specs=P(None, "gx", "gy", "gz"),
        check_vma=False,
    )
```

time: 79.7 us -> 60.2 us (0.76)
  blocking collectives: 0 us -> 32.6 us
  starting transfers between devices: 39.8 us -> 9.48 us
  other arithmetic: 19.7 us -> 0 us
  local copies, waits for them, and re-layouts: 10.9 us -> 4.28 us
  Pallas kernels: 0 us -> 5.79 us
    all_gather x0 -> x4, blocking collectives: none -> 32.6 us  [gather(): lax.all_gather(value, axis, axis=0, tiled=False, axis_index_groups=groups)]
    ppermute x6 -> x2, starting transfers between devices: 39.8 us -> 9.48 us  [the longest x1 7.56 us: on_device(): lax.ppermute(down, 'gx', [((i + 1) % count, i) for i in range(count)])]
    add x5 -> x0, other arithmetic: 8.38 us -> none  [the longest x1 5.92 us: conductance(): total + jnp.where(region == number, conductivity[number], jnp.zeros((), c...]
    mul x4 -> x0, other arithmetic: 6.09 us -> none  [the longest x2 3.3 us: operator_shrunk(): masked = keeping * field]
    pallas_call x0 -> x4, Pallas kernels: none -> 5.79 us  [the longest x1 4.97 us: on_device(): call(stencil, f32((3, BX, BY, BZ)), 7, 1, 'stencil', scratch=(pltpu.VMEM(...]
    slice x18 -> x0, local copies, waits for them, and re-layouts: 5.55 us -> none  [the longest x2 1.75 us: with_halo(): lax.slice_in_dim(cells, cells.shape[dim] - width, cells.shape[dim], axis=...]
    unnamed x4 -> x12, local copies, waits for them, and re-layouts: 0.62 us -> 4.28 us
    concatenate x3 -> x0, other arithmetic: 2.59 us -> none  [the longest x2 1.61 us: with_halo(): jnp.concatenate([lax.ppermute(tail, axis, [(i, (i + 1) % count) for i in...]
  transfers between devices with their start and end apart: 6 -> 2, of which waited for: 5 -> 1; matrix products, arithmetic and copies ran while one was open for 2% -> 0% of each run, Pallas kernels for 0% -> 0%
where the time goes in v1:
time: 60.2 us; the launch traced here: 59.9 us
  blocking collectives  32.6 us (54%)
  starting transfers between devices  9.48 us (16%)
  waiting for transfers between devices  7.69 us (13%)
  Pallas kernels  5.79 us (10%)
  local copies, waits for them, and re-layouts  4.28 us (7%)
    all_gather x4, blocking collectives, gather(): lax.all_gather(value, axis, axis=0, tiled=False, axis_index_groups=groups)  32.6 us
    ppermute x1, waiting for transfers between devices, on_device(): low = lax.ppermute(up, 'gx', [(i, (i + 1) % count) for i in range(count)])  7.69 us
    ppermute x1, starting transfers between devices, on_device(): lax.ppermute(down, 'gx', [((i + 1) % count, i) for i in range(count)])  7.56 us
    pallas_call x1, Pallas kernels, on_device(): call(stencil, f32((3, BX, BY, BZ)), 7, 1, 'stencil', scratch=(pltpu.VMEM(...  4.97 us
    unnamed x12, local copies, waits for them, and re-layouts  4.28 us
    ppermute x1, starting transfers between devices, on_device(): low = lax.ppermute(up, 'gx', [(i, (i + 1) % count) for i in range(count)])  1.92 us
  transfers between devices with their start and end apart: 2, of which 1 were waited for; matrix products, arithmetic and copies ran while one was open for 0% of the time, Pallas kernels for 0%

profile of v1, /device:TPU:1, one launch (start us, length us, event | category | flops | bytes accessed | tf_op | source)
XLA Modules:
  0.0 59.9 jit_solution(14771550691115020935)
XLA Ops:
  0.0 0.0 copy-start.5
  0.0 0.7 %copy-done.5 = f32[8]{0:T(128)S(1)} copy-done((f32[8]{0:T(128)S(1)}, f32[8]{0:T(128)}, u32[]{:S(2)}) %copy-start.5) | copy-done | bytes 56
  0.7 0.0 copy-start
  0.7 0.9 %copy-done = f32[3,8,16,128]{3,2,1,0:T(8,128)S(1)} copy-done((f32[3,8,16,128]{3,2,1,0:T(8,128)S(1)}, f32[3,8,16,128]{3,2,1,0:T(8,128)}, u32[]{:S(2)}) %copy-start) | copy-done | bytes 196632
  1.6 0.0 copy-start.2
  1.6 0.9 %copy-done.2 = f32[3,8,16,128]{3,2,1,0:T(8,128)S(1)} copy-done((f32[3,8,16,128]{3,2,1,0:T(8,128)S(1)}, f32[3,8,16,128]{3,2,1,0:T(8,128)}, u32[]{:S(2)}) %copy-start.2) | copy-done | bytes 196632
  2.5 0.0 copy-start.3
  2.5 0.9 %copy-done.3 = s32[3,8,16,128]{3,2,1,0:T(8,128)S(1)} copy-done((s32[3,8,16,128]{3,2,1,0:T(8,128)S(1)}, s32[3,8,16,128]{3,2,1,0:T(8,128)}, u32[]{:S(2)}) %copy-start.3) | copy-done | bytes 196632
  3.4 0.0 copy-start.4
  3.4 0.8 %copy-done.4 = s32[8,16,128]{2,1,0:T(8,128)S(1)} copy-done((s32[8,16,128]{2,1,0:T(8,128)S(1)}, s32[8,16,128]{2,1,0:T(8,128)}, u32[]{:S(2)}) %copy-start.4) | copy-done | bytes 65560
  4.3 0.7 %prepare.1 = (f32[3,8,16,128]{3,2,1,0:T(8,128)S(1)}, f32[8,8,128]{2,1,0:T(8,128)S(1)}) custom-call(f32[8]{0:T(128)S(1)} %copy-done.5, f32[3,8,16,128]{3,2,1,0:T(8,128)S(1)} %copy-done, f32[3,8,16,128]{3,2,1,0:T(8,128)S(1)} %copy-done.2, s32[8,16,128]{2,1,0:T(8,128)S(1)} %copy-done.4, s32[3,8,16,128]{3,2,1,0:T(8,128)S(1)} %copy-done.3), custom_call_target="tpu_custom_call" | custom-call | flops 1000000 | bytes 1000000 | tf_op jit(solution)/shard_map/prepare/pallas_call | solution.py:244
  5.0 0.0 copy-start.1
  5.0 5.0 %all-gather = f32[16,8,128]{2,1,0:T(8,128)S(1)} all-gather(f32[8,8,128]{2,1,0:T(8,128)S(1)} %get-tuple-element.13), channel_id=2, replica_groups={{0,1},{2,3},{4,5},{6,7},{8,9},{10,11},{12,13},{14,15},{16,17},{18,19},{..., dimensions={0}, use_global_device_ids=true | all-gather | bytes 98304 | tf_op jit(solution)/shard_map/all_gather | solution.py:236
  10.0 13.7 %all-gather.1 = f32[16,8,128]{2,1,0:T(8,128)S(1)} all-gather(f32[8,8,128]{2,1,0:T(8,128)S(1)} %get-tuple-element.13), channel_id=3, replica_groups={{1,2},{3,4},{5,6},{7,8},{9,10},{11,0},{13,14},{15,16},{17,18},{19,20},{..., dimensions={0}, use_global_device_ids=true | all-gather | bytes 98304 | tf_op jit(solution)/shard_map/all_gather | solution.py:236
  23.7 0.0 copy-done.1
  23.8 7.6 %collective-permute-start.1 = (f32[4,104,128]{2,1,0:T(8,128)S(1)}, f32[4,104,128]{2,1,0:T(8,128)S(1)}, u32[]{:S(2)}, u32[]{:S(2)}) collective-permute-start(f32[4,104,128]{2,1,0:T(8,128)S(1)} %get-tuple-element.16), channel_id=1, source_target_pairs={{48,0},{96,48},{144,96},{192,144},{240,192},{288,240},{336,288},{3... | collective-permute-start | bytes 638984 | tf_op jit(solution)/shard_map/ppermute | solution.py:256
  31.3 1.9 %collective-permute-start = (f32[3,104,128]{2,1,0:T(8,128)S(1)}, f32[3,104,128]{2,1,0:T(8,128)S(1)}, u32[]{:S(2)}, u32[]{:S(2)}) collective-permute-start(f32[3,104,128]{2,1,0:T(8,128)S(1)} %get-tuple-element.15), channel_id=1, source_target_pairs={{0,48},{48,96},{96,144},{144,192},{192,240},{240,288},{288,336},{3... | collective-permute-start | bytes 479240 | tf_op jit(solution)/shard_map/ppermute | solution.py:255
  33.3 7.7 %collective-permute-done.low = f32[3,104,128]{2,1,0:T(8,128)S(1)} collective-permute-done((f32[3,104,128]{2,1,0:T(8,128)S(1)}, f32[3,104,128]{2,1,0:T(8,128)S(1)}, u32[]{:S(2)}, u32[]{:S(2)}) %collective-permute-start) | collective-permute-done | bytes 159776 | tf_op jit(solution)/shard_map/ppermute | solution.py:255
  41.0 0.0 collective-permute-done.1.high
  41.0 0.1 send_y.1
  41.0 5.9 %all-gather.2 = f32[848,128]{1,0:T(8,128)S(1)} all-gather(f32[424,128]{1,0:T(8,128)S(1)} %get-tuple-element.17), channel_id=4, replica_groups={{0,12},{24,36},{1,13},{25,37},{2,14},{26,38},{3,15},{27,39},{4,16},{28,..., dimensions={0}, use_global_device_ids=true | all-gather | bytes 651264 | tf_op jit(solution)/shard_map/all_gather | solution.py:236
  46.9 8.0 %all-gather.3 = f32[848,128]{1,0:T(8,128)S(1)} all-gather(f32[424,128]{1,0:T(8,128)S(1)} %get-tuple-element.18), channel_id=5, replica_groups={{12,24},{36,0},{13,25},{37,1},{14,26},{38,2},{15,27},{39,3},{16,28},{40..., dimensions={0}, use_global_device_ids=true | all-gather | bytes 651264 | tf_op jit(solution)/shard_map/all_gather | solution.py:236
  54.9 5.0 %stencil.1 = f32[3,8,16,128]{3,2,1,0:T(8,128)} custom-call(s32[1]{0:T(128)} %bitcast.ypar, f32[3,8,16,128]{3,2,1,0:T(8,128)S(1)} %copy-done.1, f32[3,8,16,128]{3,2,1,0:T(8,128)S(1)} %get-tuple-element.12.sigma, f32[8,8,128]{2,1,0:T(8,128)S(1)} %get-tuple-element.14.packed, f32[3,104,128]{2,1,0:T(8,128)S(1)} %collective-permute-done.low, ...), custom_call_target="tpu_custom_call" | custom-call | flops 1000000 | bytes 1000000 | tf_op jit(solution)/shard_map/stencil/pallas_call | solution.py:266
  (1 shorter events, 0.0 us)
Async XLA Ops:
  0.0 0.7 %copy-start.5 = (f32[8]{0:T(128)S(1)}, f32[8]{0:T(128)}, u32[]{:S(2)}) copy-start(f32[8]{0:T(128)} %cond.1) | copy-start | bytes 100
  0.7 0.9 %copy-start = (f32[3,8,16,128]{3,2,1,0:T(8,128)S(1)}, f32[3,8,16,128]{3,2,1,0:T(8,128)}, u32[]{:S(2)}) copy-start(f32[3,8,16,128]{3,2,1,0:T(8,128)} %rhs.7) | copy-start | bytes 589828
  1.6 0.9 %copy-start.2 = (f32[3,8,16,128]{3,2,1,0:T(8,128)S(1)}, f32[3,8,16,128]{3,2,1,0:T(8,128)}, u32[]{:S(2)}) copy-start(f32[3,8,16,128]{3,2,1,0:T(8,128)} %fraction.1) | copy-start | bytes 589828
  2.5 0.9 %copy-start.3 = (s32[3,8,16,128]{3,2,1,0:T(8,128)S(1)}, s32[3,8,16,128]{3,2,1,0:T(8,128)}, u32[]{:S(2)}) copy-start(s32[3,8,16,128]{3,2,1,0:T(8,128)} %flags.1) | copy-start | bytes 589828
  3.4 0.8 %copy-start.4 = (s32[8,16,128]{2,1,0:T(8,128)S(1)}, s32[8,16,128]{2,1,0:T(8,128)}, u32[]{:S(2)}) copy-start(s32[8,16,128]{2,1,0:T(8,128)} %region.1) | copy-start | bytes 196612
  5.0 18.7 %copy-start.1 = (f32[3,8,16,128]{3,2,1,0:T(8,128)S(1)}, f32[3,8,16,128]{3,2,1,0:T(8,128)}, u32[]{:S(2)}) copy-start(f32[3,8,16,128]{3,2,1,0:T(8,128)} %rhs.7) | copy-start | bytes 589828
  23.8 17.2 %collective-permute-start.1 = (f32[4,104,128]{2,1,0:T(8,128)S(1)}, f32[4,104,128]{2,1,0:T(8,128)S(1)}, u32[]{:S(2)}, u32[]{:S(2)}) collective-permute-start(f32[4,104,128]{2,1,0:T(8,128)S(1)} %get-tuple-element.16), channel_id=1, source_target_pairs={{48,0},{96,48},{144,96},{192,144},{240,192},{288,240},{336,288},{3... | collective-permute-start | bytes 638984 | tf_op jit(solution)/shard_map/ppermute | solution.py:256
  31.3 9.6 %collective-permute-start = (f32[3,104,128]{2,1,0:T(8,128)S(1)}, f32[3,104,128]{2,1,0:T(8,128)S(1)}, u32[]{:S(2)}, u32[]{:S(2)}) collective-permute-start(f32[3,104,128]{2,1,0:T(8,128)S(1)} %get-tuple-element.15), channel_id=1, source_target_pairs={{0,48},{48,96},{96,144},{144,192},{192,240},{240,288},{288,336},{3... | collective-permute-start | bytes 479240 | tf_op jit(solution)/shard_map/ppermute | solution.py:255

commit v2 on v1

v2 whole, which is shorter than its diff:
```python
import functools

import jax
import jax.numpy as jnp
import numpy as np
from jax import lax
from jax.experimental import pallas as pl
from jax.experimental.pallas import tpu as pltpu
from jax.sharding import PartitionSpec as P

EDGE = 0.8
NODE = 0.8 / 7.0

BX, BY, BZ = 8, 16, 128
LOW, HIGH = 3, 4
EXT = LOW + BX + HIGH
VMEM_LIMIT = 16 * 1024 * 1024

VMEM = pl.BlockSpec(memory_space=pltpu.VMEM)
SMEM = pl.BlockSpec(memory_space=pltpu.SMEM)
HBM = pl.BlockSpec(memory_space=pltpu.HBM)


def halo_need():
    size = BX + 9

    def at(need, axis, k):
        return np.roll(need, k, axis)

    out = np.zeros((3, size, size, size), bool)
    out[:, 4 : 4 + BX, 4 : 4 + BX, 4 : 4 + BX] = True
    node = np.zeros((4, size, size, size), bool)
    for a in range(3):
        both = out[a] | at(out[a], a, 1)
        node[0] |= both
        node[a + 1] |= both
    near = node.copy()
    for a in range(3):
        near |= np.roll(node, 1, a + 1) | np.roll(node, -1, a + 1)
    masked = np.stack([near[0] | at(near[0], a, -1) | near[a + 1] | at(near[a + 1], a, -1) for a in range(3)])

    def operand(need):
        face = np.zeros_like(need)
        for a in range(3):
            b, c = (a + 1) % 3, (a + 2) % 3
            face[b] |= need[a] | at(need[a], c, -1)
            face[c] |= need[a] | at(need[a], b, -1)
        edge = need.copy()
        for a in range(3):
            b, c = (a + 1) % 3, (a + 2) % 3
            edge[b] |= face[a] | at(face[a], c, 1)
            edge[c] |= face[a] | at(face[a], b, 1)
        return edge

    second = operand(masked) | out
    first = operand(second)
    return second.any(3).astype(int) + first.any(3).astype(int)


NEED = halo_need()


def plane_need(c, p):
    return NEED[c, p - LOW + 4].max()


def row_counts(c, p):
    need = NEED[c, p - LOW + 4]
    below, above = need[:4], need[4 + BX :]
    return tuple((int((side > 0).sum()), int((side > 1).sum())) for side in (below, above))


def x_layout(planes):
    at, rows = {}, 0
    for p in planes:
        for field in range(6):
            if plane_need(field % 3, p) > field // 3:
                at[p, field] = rows
                rows += BY
    for p in planes:
        at[p, "packed"] = rows
        rows += 8
    return at, rows


X_LOW, X_LOW_ROWS = x_layout(range(LOW))
X_HIGH, X_HIGH_ROWS = x_layout(range(LOW + BX, EXT))


def y_layout(side):
    at, rows = {}, 0
    for p in range(EXT):
        for field in range(6):
            count = row_counts(field % 3, p)[side][field // 3]
            at[p, field] = (rows, count)
            rows += count
    rows = -(-rows // 8) * 8
    for p in range(0, EXT, 2):
        at[p, "packed"] = at[p + 1, "packed"] = rows
        rows += 4
    return at, rows


Y_LOW, Y_LOW_ROWS = y_layout(0)
Y_HIGH, Y_HIGH_ROWS = y_layout(1)
Y_ROWS = -(-max(Y_LOW_ROWS, Y_HIGH_ROWS) // 8) * 8


def call(body, out_shape, specs, name, scratch=(), flops=1000000):
    return pl.pallas_call(
        body,
        out_shape=out_shape,
        in_specs=specs,
        out_specs=jax.tree.map(lambda _: VMEM, out_shape),
        scratch_shapes=list(scratch),
        compiler_params=pltpu.CompilerParams(vmem_limit_bytes=VMEM_LIMIT),
        cost_estimate=pl.CostEstimate(flops=flops, bytes_accessed=1000000, transcendentals=0),
        name=name,
    )


def lanes(shape):
    return lax.broadcasted_iota(jnp.int32, shape, 1)


def rotate(v, shift, axis):
    return pltpu.roll(v, shift % v.shape[axis], axis)


def weigh(sigma):
    return jnp.where(sigma > 0.0, EDGE / (4.0 + sigma), 0.0)


def prepare(cond_in, rhs_in, fraction_in, region_in, flags_in, rhs, sigma, first_iter, packed_out, cond, fraction, region, flags, sems):
    copies = [
        pltpu.make_async_copy(source, target, sems.at[i])
        for i, (source, target) in enumerate(
            ((cond_in, cond), (region_in, region), (fraction_in, fraction), (flags_in, flags), (rhs_in, rhs))
        )
    ]
    for copy in copies:
        copy.start()
    for copy in copies:
        copy.wait()
    group = lanes((8, BZ)) // 8
    for x in range(BX):
        where = region[x]
        conductivity = jnp.full((BY, BZ), cond[0], jnp.float32)
        for number in range(1, 8):
            conductivity = jnp.where(where == number, cond[number], conductivity)
        packed = jnp.zeros((8, BZ), jnp.float32)
        for field in range(6):
            if field < 3:
                value = rhs[field, x]
            else:
                c = field - 3
                value = jnp.where(flags[c, x] == 0, conductivity * fraction[c, x], 0.0)
                sigma[c, x] = value
                first_iter[c, x] = weigh(value) * rhs[c, x]
            for tile in range(2):
                slot = field * 2 + tile
                moved = rotate(value[tile * 8 : tile * 8 + 8], LOW + 8 * slot, 1)
                packed = jnp.where(group == slot, moved, packed)
        packed_out[x] = packed


def send_x(zpar, rhs, sigma, first_iter, first, second, up_out, down_out, packed_out):
    even = zpar[0] == 0
    below = (lanes((8, BZ)) % 8) < LOW
    for x in range(BX):
        from_high = jnp.where(even, first[1, x], second[1, x])
        from_low = jnp.where(even, second[0, x], first[0, x])
        packed_out[x] = jnp.where(below, from_low, from_high)
    for out, layout, shift in ((up_out, X_LOW, BX), (down_out, X_HIGH, -BX)):
        for (p, field), at in layout.items():
            x = p - LOW + shift
            if field == "packed":
                out[at : at + 8] = packed_out[x]
            elif field >= 3:
                out[at : at + BY] = sigma[field - 3, x]
            else:
                out[at : at + BY] = (rhs if plane_need(field, p) == 2 else first_iter)[field, x]


def plane_rows(p, field, start, stop, rhs, sigma, low, high):
    if p < LOW:
        at = X_LOW[p, field]
        return low[at + start : at + stop]
    if p >= LOW + BX:
        at = X_HIGH[p, field]
        return high[at + start : at + stop]
    return (rhs if field < 3 else sigma)[field % 3, p - LOW, start:stop]


def plane_packed(p, start, stop, packed, low, high):
    if p < LOW:
        at = X_LOW[p, "packed"]
        return low[at + start : at + stop]
    if p >= LOW + BX:
        at = X_HIGH[p, "packed"]
        return high[at + start : at + stop]
    return packed[p - LOW, start:stop]


def send_y(ypar, rhs, sigma, first_iter, packed, low, high, first_out, second_out):
    swap = (lanes((4, BZ)) // 8) % 2

    def first_rows(p, c, start, stop):
        if LOW <= p < LOW + BX:
            return first_iter[c, p - LOW, start:stop]
        value = plane_rows(p, c, start, stop, rhs, sigma, low, high)
        if plane_need(c, p) == 2:
            value = weigh(plane_rows(p, c + 3, start, stop, rhs, sigma, low, high)) * value
        return value

    def fill(out, layout, side):
        for p in range(EXT):
            for field in range(6):
                at, count = layout[p, field]
                both = layout[p, field % 3 + 3][1]
                if field >= 3 and count:
                    start = 0 if side else BY - count
                    out[at : at + count] = plane_rows(p, field, start, start + count, rhs, sigma, low, high)
                if field < 3 and both:
                    start = 0 if side else BY - both
                    place = at if side else at + count - both
                    out[place : place + both] = plane_rows(p, field, start, start + both, rhs, sigma, low, high)
                if field < 3 and count > both:
                    start = both if side else BY - count
                    place = at + both if side else at
                    out[place : place + count - both] = first_rows(p, field, start, start + count - both)
        start = 0 if side else 4
        for p in range(0, EXT, 2):
            value = plane_packed(p, start, start + 4, packed, low, high)
            if p + 1 < EXT:
                other = plane_packed(p + 1, start, start + 4, packed, low, high)
                value = jnp.where(swap == 1 - side, value, rotate(other, 8 if side else -8, 1))
            at = layout[p, "packed"]
            out[at : at + 4] = value

    @pl.when(ypar[0] == 0)
    def _():
        fill(first_out, Y_LOW, 0)
        fill(second_out, Y_HIGH, 1)

    @pl.when(ypar[0] != 0)
    def _():
        fill(second_out, Y_LOW, 0)
        fill(first_out, Y_HIGH, 1)


def up_y(v):
    return rotate(v, -1, 0)


def down_y(v):
    return rotate(v, 1, 0)


def up_z(v):
    return rotate(v, -1, 1)


def down_z(v):
    return rotate(v, 1, 1)


def stencil(ypar, rhs, sigma, first_iter, packed, low, high, first, second, out, wide, weight, iterate, second_iter, nodal):
    even = ypar[0] == 0
    row8 = lax.broadcasted_iota(jnp.int32, (8, BZ), 0)

    for p in range(EXT):
        at_low, at_high = Y_LOW[p, "packed"], Y_HIGH[p, "packed"]
        edge = jnp.concatenate(
            [
                jnp.where(even, first[1, at_high : at_high + 4], second[1, at_high : at_high + 4]),
                jnp.where(even, second[0, at_low : at_low + 4], first[0, at_low : at_low + 4]),
            ],
            axis=0,
        )
        edge = jnp.where((row8 < 4) == (p % 2 == 0), edge, rotate(edge, -8, 1))
        whole = plane_packed(p, 0, 8, packed, low, high)
        for field in range(6):
            c = field % 3
            if plane_need(c, p) == 0:
                continue
            if plane_need(c, p) > field // 3:
                wide[field, p, 0:BY, 0:BZ] = plane_rows(p, field, 0, BY, rhs, sigma, low, high)
                at, count = Y_HIGH[p, field]
                if count:
                    wide[field, p, BY : BY + count, 0:BZ] = jnp.where(
                        even, first[1, at : at + count], second[1, at : at + count]
                    )
                at, count = Y_LOW[p, field]
                if count:
                    wide[field, p, 24 - count : 24, 0:BZ] = jnp.where(
                        even, second[0, at : at + count], first[0, at : at + count]
                    )
            wide[field, p, 0:8, BZ:] = rotate(whole, -(LOW + 16 * field), 1)
            wide[field, p, 8:16, BZ:] = rotate(whole, -(LOW + 16 * field + 8), 1)
            wide[field, p, 16:24, BZ:] = rotate(edge, -(LOW + 16 * field), 1)
        for c in range(3):
            if plane_need(c, p) == 0:
                continue
            if plane_need(c, p) == 1:
                iterate[c, p, :, 0:BZ] = wide[c, p, :, 0:BZ]
                iterate[c, p, :, BZ:] = weigh(wide[3 + c, p, :, BZ:]) * wide[c, p, :, BZ:]
                continue
            w = weigh(wide[3 + c, p])
            weight[c, p] = w
            iterate[c, p] = w * wide[c, p]
            (low_any, low_both), (high_any, high_both) = row_counts(c, p)
            for start, stop in ((BY + high_both, BY + high_any), (24 - low_any, 24 - low_both)):
                if start < stop:
                    iterate[c, p, start:stop, 0:BZ] = wide[c, p, start:stop, 0:BZ]

    def faces(u, p):
        u0, u1, u2 = u[0, p], u[1, p], u[2, p]
        f0 = (up_y(u2) - u2) - (up_z(u1) - u1)
        f1 = (up_z(u0) - u0) - (u[2, p + 1] - u2)
        f2 = (u[1, p + 1] - u1) - (up_y(u0) - u0)
        return f0, f1, f2

    def curl0(f):
        return (down_z(f[1]) - f[1]) - (down_y(f[2]) - f[2])

    def curl1(f, prev):
        return (prev[2] - f[2]) - (down_z(f[0]) - f[0])

    def curl2(f, prev):
        return (down_y(f[0]) - f[0]) - (prev[1] - f[1])

    prev = faces(iterate, 0)
    for p in range(1, EXT - 1):
        f = faces(iterate, p)
        for c, k in enumerate((curl0(f), curl1(f, prev), curl2(f, prev))):
            u = iterate[c, p]
            second_iter[c, p] = u + weight[c, p] * (wide[c, p] - (k + wide[3 + c, p] * u))
        prev = f

    def residual(c, p, k):
        s = wide[3 + c, p]
        return jnp.where(s > 0.0, wide[c, p] - (k + s * second_iter[c, p]), 0.0)

    prev = faces(second_iter, 1)
    before = residual(0, 1, curl0(prev))
    for p in range(2, EXT - 2):
        f = faces(second_iter, p)
        q0 = residual(0, p, curl0(f))
        q1 = residual(1, p, curl1(f, prev))
        q2 = residual(2, p, curl2(f, prev))
        d1, d2 = down_y(q1), down_z(q2)
        nodal[0, p] = (before - q0) + (d1 - q1) + (d2 - q2)
        nodal[1, p] = (before + q0) * 0.5
        nodal[2, p] = (d1 + q1) * 0.5
        nodal[3, p] = (d2 + q2) * 0.5
        prev, before = f, q0

    def node(c, p):
        b = nodal[c, p]
        near = (nodal[c, p - 1] + nodal[c, p + 1]) + (up_y(b) + down_y(b)) + (up_z(b) + down_z(b))
        return (1.2 * NODE) * b + (NODE * NODE) * near

    n0, n1 = node(0, LOW), node(1, LOW)
    for x in range(BX):
        p = x + LOW
        n0_next, n1_next = node(0, p + 1), node(1, p + 1)
        n2, n3 = node(2, p), node(3, p)
        corrections = (
            (n0_next - n0) + (n1_next + n1) * 0.5,
            (up_y(n0) - n0) + (n2 + up_y(n2)) * 0.5,
            (up_z(n0) - n0) + (n3 + up_z(n3)) * 0.5,
        )
        for c in range(3):
            kept = second_iter[c, p, 0:BY, 0:BZ] + corrections[c][0:BY, 0:BZ]
            out[c, x] = jnp.where(sigma[c, x] > 0.0, kept, 0.96 * rhs[c, x])
        n0, n1 = n0_next, n1_next


def pairs(count):
    return (
        [[i, i + 1] for i in range(0, count, 2)],
        [[i, (i + 1) % count] for i in range(1, count, 2)],
    )


def gather(value, axis, groups):
    return lax.all_gather(value, axis, axis=0, tiled=False, axis_index_groups=groups)


def on_device(rhs, conductivity, fraction, region, flags):
    f32 = functools.partial(jax.ShapeDtypeStruct, dtype=jnp.float32)
    parity = lambda axis: (lax.axis_index(axis) % 2).astype(jnp.int32).reshape(1)
    ypar, zpar = parity("gy"), parity("gz")

    block = f32((3, BX, BY, BZ))
    rhs, sigma, first_iter, packed = call(
        prepare,
        (block, block, block, f32((BX, 8, BZ))),
        [HBM] * 5,
        "prepare",
        scratch=(
            pltpu.SMEM((8,), jnp.float32),
            pltpu.VMEM((3, BX, BY, BZ), jnp.float32),
            pltpu.VMEM((BX, BY, BZ), jnp.int32),
            pltpu.VMEM((3, BX, BY, BZ), jnp.int32),
            pltpu.SemaphoreType.DMA((5,)),
        ),
    )(conductivity, rhs, fraction, region, flags)
    even_z, odd_z = pairs(lax.axis_size("gz"))
    first = gather(packed, "gz", even_z)
    second = gather(packed, "gz", odd_z)

    up, down, packed = call(
        send_x, (f32((X_LOW_ROWS, BZ)), f32((X_HIGH_ROWS, BZ)), f32((BX, 8, BZ))), [SMEM] + [VMEM] * 5, "send_x"
    )(zpar, rhs, sigma, first_iter, first, second)
    count = lax.axis_size("gx")
    low = lax.ppermute(up, "gx", [(i, (i + 1) % count) for i in range(count)])
    high = lax.ppermute(down, "gx", [((i + 1) % count, i) for i in range(count)])

    even_y, odd_y = pairs(lax.axis_size("gy"))
    to_first, to_second = call(
        send_y, (f32((Y_ROWS, BZ)), f32((Y_ROWS, BZ))), [SMEM] + [VMEM] * 6, "send_y"
    )(ypar, rhs, sigma, first_iter, packed, low, high)
    first = gather(to_first, "gy", even_y)
    second = gather(to_second, "gy", odd_y)

    wide = (EXT, 24, 2 * BZ)
    return call(
        stencil,
        block,
        [SMEM] + [VMEM] * 8,
        "stencil",
        scratch=(
            pltpu.VMEM((6, *wide), jnp.float32),
            pltpu.VMEM((3, *wide), jnp.float32),
            pltpu.VMEM((3, *wide), jnp.float32),
            pltpu.VMEM((3, *wide), jnp.float32),
            pltpu.VMEM((4, *wide), jnp.float32),
        ),
    )(ypar, rhs, sigma, first_iter, packed, low, high, first, second)


def solution(mesh):
    return jax.shard_map(
        on_device,
        mesh=mesh,
        in_specs=(
            P(None, "gx", "gy", "gz"),
            P(),
            P(None, "gx", "gy", "gz"),
            P("gx", "gy", "gz"),
            P(None, "gx", "gy", "gz"),
        ),
        out_specs=P(None, "gx", "gy", "gz"),
        check_vma=False,
    )
```

time: 60.2 us -> 58.2 us (0.967)
  blocking collectives: 32.6 us -> 30.4 us
    all_gather x4, blocking collectives: 32.6 us -> 30.4 us  [gather(): lax.all_gather(value, axis, axis=0, tiled=False, axis_index_groups=groups)]
    unnamed x12 -> x10, local copies, waits for them, and re-layouts: 4.28 us -> 4.27 us
where the time goes in v2:
time: 58.2 us; the launch traced here: 57.9 us
  blocking collectives  30.4 us (52%)
  starting transfers between devices  9.48 us (16%)
  waiting for transfers between devices  7.43 us (13%)
  Pallas kernels  6.28 us (11%)
  local copies, waits for them, and re-layouts  4.27 us (7%)
    all_gather x4, blocking collectives, gather(): lax.all_gather(value, axis, axis=0, tiled=False, axis_index_groups=groups)  30.4 us
    ppermute x1, starting transfers between devices, on_device(): lax.ppermute(down, 'gx', [((i + 1) % count, i) for i in range(count)])  7.56 us
    ppermute x1, waiting for transfers between devices, on_device(): low = lax.ppermute(up, 'gx', [(i, (i + 1) % count) for i in range(count)])  7.43 us
    pallas_call x1, Pallas kernels, on_device(): call(stencil, block, [SMEM] + [VMEM] * 8, 'stencil', scratch=(pltpu.VMEM(...  5.09 us
    unnamed x10, local copies, waits for them, and re-layouts  4.27 us
    ppermute x1, starting transfers between devices, on_device(): low = lax.ppermute(up, 'gx', [(i, (i + 1) % count) for i in range(count)])  1.92 us
  transfers between devices with their start and end apart: 2, of which 1 were waited for; matrix products, arithmetic and copies ran while one was open for 0% of the time, Pallas kernels for 0%

profile of v2, /device:TPU:1, one launch (start us, length us, event | category | flops | bytes accessed | tf_op | source)
XLA Modules:
  0.0 57.9 jit_solution(14834984842641816294)
XLA Ops:
  0.0 0.0 copy-start.4
  0.0 0.7 %copy-done.4 = f32[8]{0:T(128)S(1)} copy-done((f32[8]{0:T(128)S(1)}, f32[8]{0:T(128)}, u32[]{:S(2)}) %copy-start.4) | copy-done | bytes 56
  0.7 0.0 copy-start
  0.7 0.9 %copy-done = f32[3,8,16,128]{3,2,1,0:T(8,128)S(1)} copy-done((f32[3,8,16,128]{3,2,1,0:T(8,128)S(1)}, f32[3,8,16,128]{3,2,1,0:T(8,128)}, u32[]{:S(2)}) %copy-start) | copy-done | bytes 196632
  1.6 0.0 copy-start.1
  1.6 0.9 %copy-done.1 = f32[3,8,16,128]{3,2,1,0:T(8,128)S(1)} copy-done((f32[3,8,16,128]{3,2,1,0:T(8,128)S(1)}, f32[3,8,16,128]{3,2,1,0:T(8,128)}, u32[]{:S(2)}) %copy-start.1) | copy-done | bytes 196632
  2.5 0.0 copy-start.2
  2.5 0.9 %copy-done.2 = s32[3,8,16,128]{3,2,1,0:T(8,128)S(1)} copy-done((s32[3,8,16,128]{3,2,1,0:T(8,128)S(1)}, s32[3,8,16,128]{3,2,1,0:T(8,128)}, u32[]{:S(2)}) %copy-start.2) | copy-done | bytes 196632
  3.4 0.0 copy-start.3
  3.4 0.8 %copy-done.3 = s32[8,16,128]{2,1,0:T(8,128)S(1)} copy-done((s32[8,16,128]{2,1,0:T(8,128)S(1)}, s32[8,16,128]{2,1,0:T(8,128)}, u32[]{:S(2)}) %copy-start.3) | copy-done | bytes 65560
  4.3 1.0 %prepare.1 = (f32[3,8,16,128]{3,2,1,0:T(8,128)S(1)}, f32[3,8,16,128]{3,2,1,0:T(8,128)S(1)}, f32[3,8,16,128]{3,2,1,0:T(8,128)S(1)}, f32[8,8,128]{2,1,0:T(8,128)S(1)}) custom-call(f32[8]{0:T(128)S(1)} %copy-done.4, f32[3,8,16,128]{3,2,1,0:T(8,128)S(1)} %copy-done, f32[3,8,16,128]{3,2,1,0:T(8,128)S(1)} %copy-done.1, s32[8,16,128]{2,1,0:T(8,128)S(1)} %copy-done.3, ...), custom_call_target="tpu_custom_call" | custom-call | flops 1000000 | bytes 1000000 | tf_op jit(solution)/shard_map/prepare/pallas_call | solution.py:397
  5.3 4.9 %all-gather = f32[16,8,128]{2,1,0:T(8,128)S(1)} all-gather(f32[8,8,128]{2,1,0:T(8,128)S(1)} %get-tuple-element.17), channel_id=2, replica_groups={{0,1},{2,3},{4,5},{6,7},{8,9},{10,11},{12,13},{14,15},{16,17},{18,19},{..., dimensions={0}, use_global_device_ids=true | all-gather | bytes 98304 | tf_op jit(solution)/shard_map/all_gather | solution.py:388
  10.2 13.7 %all-gather.1 = f32[16,8,128]{2,1,0:T(8,128)S(1)} all-gather(f32[8,8,128]{2,1,0:T(8,128)S(1)} %get-tuple-element.17), channel_id=3, replica_groups={{1,2},{3,4},{5,6},{7,8},{9,10},{11,0},{13,14},{15,16},{17,18},{19,20},{..., dimensions={0}, use_global_device_ids=true | all-gather | bytes 98304 | tf_op jit(solution)/shard_map/all_gather | solution.py:388
  23.9 7.6 %collective-permute-start.1 = (f32[336,128]{1,0:T(8,128)S(1)}, f32[336,128]{1,0:T(8,128)S(1)}, u32[]{:S(2)}, u32[]{:S(2)}) collective-permute-start(f32[336,128]{1,0:T(8,128)S(1)} %get-tuple-element.20), channel_id=1, source_target_pairs={{48,0},{96,48},{144,96},{192,144},{240,192},{288,240},{336,288},{3... | collective-permute-start | bytes 516104 | tf_op jit(solution)/shard_map/ppermute | solution.py:419
  31.5 1.9 %collective-permute-start = (f32[264,128]{1,0:T(8,128)S(1)}, f32[264,128]{1,0:T(8,128)S(1)}, u32[]{:S(2)}, u32[]{:S(2)}) collective-permute-start(f32[264,128]{1,0:T(8,128)S(1)} %get-tuple-element.19), channel_id=1, source_target_pairs={{0,48},{48,96},{96,144},{144,192},{192,240},{240,288},{288,336},{3... | collective-permute-start | bytes 405512 | tf_op jit(solution)/shard_map/ppermute | solution.py:418
  33.5 7.4 %collective-permute-done.low = f32[264,128]{1,0:T(8,128)S(1)} collective-permute-done((f32[264,128]{1,0:T(8,128)S(1)}, f32[264,128]{1,0:T(8,128)S(1)}, u32[]{:S(2)}, u32[]{:S(2)}) %collective-permute-start) | collective-permute-done | bytes 135200 | tf_op jit(solution)/shard_map/ppermute | solution.py:418
  40.9 0.0 collective-permute-done.1.high
  40.9 0.1 send_y.1
  41.0 5.8 %all-gather.2 = f32[496,128]{1,0:T(8,128)S(1)} all-gather(f32[248,128]{1,0:T(8,128)S(1)} %get-tuple-element.21), channel_id=4, replica_groups={{0,12},{24,36},{1,13},{25,37},{2,14},{26,38},{3,15},{27,39},{4,16},{28,..., dimensions={0}, use_global_device_ids=true | all-gather | bytes 380928 | tf_op jit(solution)/shard_map/all_gather | solution.py:388
  46.8 6.0 %all-gather.3 = f32[496,128]{1,0:T(8,128)S(1)} all-gather(f32[248,128]{1,0:T(8,128)S(1)} %get-tuple-element.22), channel_id=5, replica_groups={{12,24},{36,0},{13,25},{37,1},{14,26},{38,2},{15,27},{39,3},{16,28},{40..., dimensions={0}, use_global_device_ids=true | all-gather | bytes 380928 | tf_op jit(solution)/shard_map/all_gather | solution.py:388
  52.8 5.1 %stencil.1 = f32[3,8,16,128]{3,2,1,0:T(8,128)} custom-call(s32[1]{0:T(128)} %bitcast.ypar, f32[3,8,16,128]{3,2,1,0:T(8,128)S(1)} %get-tuple-element.14.rhs, f32[3,8,16,128]{3,2,1,0:T(8,128)S(1)} %get-tuple-element.15.sigma, f32[3,8,16,128]{3,2,1,0:T(8,128)S(1)} %get-tuple-element.16.first_iter, f32[8,8,128]{2,1,0:T(8,128)S(1)} %get-tuple-element.18.packed, ...), custom_call_target="tpu_custom_call" | custom-call | flops 1000000 | bytes 1000000 | tf_op jit(solution)/shard_map/stencil/pallas_call | solution.py:429
  (1 shorter events, 0.0 us)
Async XLA Ops:
  0.0 0.7 %copy-start.4 = (f32[8]{0:T(128)S(1)}, f32[8]{0:T(128)}, u32[]{:S(2)}) copy-start(f32[8]{0:T(128)} %cond_in.1) | copy-start | bytes 100
  0.7 0.9 %copy-start = (f32[3,8,16,128]{3,2,1,0:T(8,128)S(1)}, f32[3,8,16,128]{3,2,1,0:T(8,128)}, u32[]{:S(2)}) copy-start(f32[3,8,16,128]{3,2,1,0:T(8,128)} %rhs_in.1) | copy-start | bytes 589828
  1.6 0.9 %copy-start.1 = (f32[3,8,16,128]{3,2,1,0:T(8,128)S(1)}, f32[3,8,16,128]{3,2,1,0:T(8,128)}, u32[]{:S(2)}) copy-start(f32[3,8,16,128]{3,2,1,0:T(8,128)} %fraction_in.1) | copy-start | bytes 589828
  2.5 0.9 %copy-start.2 = (s32[3,8,16,128]{3,2,1,0:T(8,128)S(1)}, s32[3,8,16,128]{3,2,1,0:T(8,128)}, u32[]{:S(2)}) copy-start(s32[3,8,16,128]{3,2,1,0:T(8,128)} %flags_in.1) | copy-start | bytes 589828
  3.4 0.8 %copy-start.3 = (s32[8,16,128]{2,1,0:T(8,128)S(1)}, s32[8,16,128]{2,1,0:T(8,128)}, u32[]{:S(2)}) copy-start(s32[8,16,128]{2,1,0:T(8,128)} %region_in.1) | copy-start | bytes 196612
  23.9 16.9 %collective-permute-start.1 = (f32[336,128]{1,0:T(8,128)S(1)}, f32[336,128]{1,0:T(8,128)S(1)}, u32[]{:S(2)}, u32[]{:S(2)}) collective-permute-start(f32[336,128]{1,0:T(8,128)S(1)} %get-tuple-element.20), channel_id=1, source_target_pairs={{48,0},{96,48},{144,96},{192,144},{240,192},{288,240},{336,288},{3... | collective-permute-start | bytes 516104 | tf_op jit(solution)/shard_map/ppermute | solution.py:419
  31.5 9.4 %collective-permute-start = (f32[264,128]{1,0:T(8,128)S(1)}, f32[264,128]{1,0:T(8,128)S(1)}, u32[]{:S(2)}, u32[]{:S(2)}) collective-permute-start(f32[264,128]{1,0:T(8,128)S(1)} %get-tuple-element.19), channel_id=1, source_target_pairs={{0,48},{48,96},{96,144},{144,192},{192,240},{240,288},{288,336},{3... | collective-permute-start | bytes 405512 | tf_op jit(solution)/shard_map/ppermute | solution.py:418

commit v3 on v2

--- a/solution.py
+++ b/solution.py
@@ -406,7 +406,7 @@
             pltpu.VMEM((3, BX, BY, BZ), jnp.int32),
             pltpu.SemaphoreType.DMA((5,)),
         ),
-    )(conductivity, rhs, fraction, region, flags)
+    )(*(pltpu.with_memory_space_constraint(a, pltpu.HBM) for a in (conductivity, rhs, fraction, region, flags)))
     even_z, odd_z = pairs(lax.axis_size("gz"))
     first = gather(packed, "gz", even_z)
     second = gather(packed, "gz", odd_z)

time: 58.2 us -> 54.1 us (0.930)
  local copies, waits for them, and re-layouts: 4.27 us -> 0 us
    unnamed x10 -> x0, local copies, waits for them, and re-layouts: 4.27 us -> none
where the time goes in v3:
time: 54.1 us; the launch traced here: 53.9 us
  blocking collectives  30.4 us (56%)
  starting transfers between devices  9.48 us (18%)
  waiting for transfers between devices  7.43 us (14%)
  Pallas kernels  6.61 us (12%)
    all_gather x4, blocking collectives, gather(): lax.all_gather(value, axis, axis=0, tiled=False, axis_index_groups=groups)  30.4 us
    ppermute x1, starting transfers between devices, on_device(): lax.ppermute(down, 'gx', [((i + 1) % count, i) for i in range(count)])  7.56 us
    ppermute x1, waiting for transfers between devices, on_device(): low = lax.ppermute(up, 'gx', [(i, (i + 1) % count) for i in range(count)])  7.43 us
    pallas_call x1, Pallas kernels, on_device(): call(stencil, block, [SMEM] + [VMEM] * 8, 'stencil', scratch=(pltpu.VMEM(...  5.09 us
    ppermute x1, starting transfers between devices, on_device(): low = lax.ppermute(up, 'gx', [(i, (i + 1) % count) for i in range(count)])  1.92 us
    pallas_call x1, Pallas kernels, on_device(): call(prepare, (block, block, block, f32((BX, 8, BZ))), [HBM] * 5, 'prepar...  1.37 us
  transfers between devices with their start and end apart: 2, of which 1 were waited for; matrix products, arithmetic and copies ran while one was open for 0% of the time, Pallas kernels for 0%

profile of v3, /device:TPU:1, one launch (start us, length us, event | category | flops | bytes accessed | tf_op | source)
XLA Modules:
  0.0 53.9 jit_solution(2277191402514752361)
XLA Ops:
  0.0 1.4 %prepare.1 = (f32[3,8,16,128]{3,2,1,0:T(8,128)S(1)}, f32[3,8,16,128]{3,2,1,0:T(8,128)S(1)}, f32[3,8,16,128]{3,2,1,0:T(8,128)S(1)}, f32[8,8,128]{2,1,0:T(8,128)S(1)}) custom-call(f32[8]{0:T(128)} %cond_in.1, f32[3,8,16,128]{3,2,1,0:T(8,128)} %rhs_in.1, f32[3,8,16,128]{3,2,1,0:T(8,128)} %fraction_in.1, s32[8,16,128]{2,1,0:T(8,128)} %region_in.1, ...), custom_call_target="tpu_custom_call" | custom-call | flops 1000000 | bytes 1000000 | tf_op jit(solution)/shard_map/prepare/pallas_call | solution.py:397
  1.4 4.9 %all-gather = f32[16,8,128]{2,1,0:T(8,128)S(1)} all-gather(f32[8,8,128]{2,1,0:T(8,128)S(1)} %get-tuple-element.17), channel_id=2, replica_groups={{0,1},{2,3},{4,5},{6,7},{8,9},{10,11},{12,13},{14,15},{16,17},{18,19},{..., dimensions={0}, use_global_device_ids=true | all-gather | bytes 98304 | tf_op jit(solution)/shard_map/all_gather | solution.py:388
  6.2 13.7 %all-gather.1 = f32[16,8,128]{2,1,0:T(8,128)S(1)} all-gather(f32[8,8,128]{2,1,0:T(8,128)S(1)} %get-tuple-element.17), channel_id=3, replica_groups={{1,2},{3,4},{5,6},{7,8},{9,10},{11,0},{13,14},{15,16},{17,18},{19,20},{..., dimensions={0}, use_global_device_ids=true | all-gather | bytes 98304 | tf_op jit(solution)/shard_map/all_gather | solution.py:388
  20.0 7.6 %collective-permute-start.1 = (f32[336,128]{1,0:T(8,128)S(1)}, f32[336,128]{1,0:T(8,128)S(1)}, u32[]{:S(2)}, u32[]{:S(2)}) collective-permute-start(f32[336,128]{1,0:T(8,128)S(1)} %get-tuple-element.20), channel_id=1, source_target_pairs={{48,0},{96,48},{144,96},{192,144},{240,192},{288,240},{336,288},{3... | collective-permute-start | bytes 516104 | tf_op jit(solution)/shard_map/ppermute | solution.py:419
  27.6 1.9 %collective-permute-start = (f32[264,128]{1,0:T(8,128)S(1)}, f32[264,128]{1,0:T(8,128)S(1)}, u32[]{:S(2)}, u32[]{:S(2)}) collective-permute-start(f32[264,128]{1,0:T(8,128)S(1)} %get-tuple-element.19), channel_id=1, source_target_pairs={{0,48},{48,96},{96,144},{144,192},{192,240},{240,288},{288,336},{3... | collective-permute-start | bytes 405512 | tf_op jit(solution)/shard_map/ppermute | solution.py:418
  29.5 7.4 %collective-permute-done.low = f32[264,128]{1,0:T(8,128)S(1)} collective-permute-done((f32[264,128]{1,0:T(8,128)S(1)}, f32[264,128]{1,0:T(8,128)S(1)}, u32[]{:S(2)}, u32[]{:S(2)}) %collective-permute-start) | collective-permute-done | bytes 135200 | tf_op jit(solution)/shard_map/ppermute | solution.py:418
  36.9 0.0 collective-permute-done.1.high
  36.9 0.1 send_y.1
  37.1 5.8 %all-gather.2 = f32[496,128]{1,0:T(8,128)S(1)} all-gather(f32[248,128]{1,0:T(8,128)S(1)} %get-tuple-element.21), channel_id=4, replica_groups={{0,12},{24,36},{1,13},{25,37},{2,14},{26,38},{3,15},{27,39},{4,16},{28,..., dimensions={0}, use_global_device_ids=true | all-gather | bytes 380928 | tf_op jit(solution)/shard_map/all_gather | solution.py:388
  42.8 6.0 %all-gather.3 = f32[496,128]{1,0:T(8,128)S(1)} all-gather(f32[248,128]{1,0:T(8,128)S(1)} %get-tuple-element.22), channel_id=5, replica_groups={{12,24},{36,0},{13,25},{37,1},{14,26},{38,2},{15,27},{39,3},{16,28},{40..., dimensions={0}, use_global_device_ids=true | all-gather | bytes 380928 | tf_op jit(solution)/shard_map/all_gather | solution.py:388
  48.8 5.1 %stencil.1 = f32[3,8,16,128]{3,2,1,0:T(8,128)} custom-call(s32[1]{0:T(128)} %bitcast.ypar, f32[3,8,16,128]{3,2,1,0:T(8,128)S(1)} %get-tuple-element.14.rhs, f32[3,8,16,128]{3,2,1,0:T(8,128)S(1)} %get-tuple-element.15.sigma, f32[3,8,16,128]{3,2,1,0:T(8,128)S(1)} %get-tuple-element.16.first_iter, f32[8,8,128]{2,1,0:T(8,128)S(1)} %get-tuple-element.18.packed, ...), custom_call_target="tpu_custom_call" | custom-call | flops 1000000 | bytes 1000000 | tf_op jit(solution)/shard_map/stencil/pallas_call | solution.py:429
  (1 shorter events, 0.0 us)
Async XLA Ops:
  20.0 16.9 %collective-permute-start.1 = (f32[336,128]{1,0:T(8,128)S(1)}, f32[336,128]{1,0:T(8,128)S(1)}, u32[]{:S(2)}, u32[]{:S(2)}) collective-permute-start(f32[336,128]{1,0:T(8,128)S(1)} %get-tuple-element.20), channel_id=1, source_target_pairs={{48,0},{96,48},{144,96},{192,144},{240,192},{288,240},{336,288},{3... | collective-permute-start | bytes 516104 | tf_op jit(solution)/shard_map/ppermute | solution.py:419
  27.6 9.4 %collective-permute-start = (f32[264,128]{1,0:T(8,128)S(1)}, f32[264,128]{1,0:T(8,128)S(1)}, u32[]{:S(2)}, u32[]{:S(2)}) collective-permute-start(f32[264,128]{1,0:T(8,128)S(1)} %get-tuple-element.19), channel_id=1, source_target_pairs={{0,48},{48,96},{96,144},{144,192},{192,240},{240,288},{288,336},{3... | collective-permute-start | bytes 405512 | tf_op jit(solution)/shard_map/ppermute | solution.py:418

commit v4 on v3

v4 whole, which is shorter than its diff:
```python
import functools

import jax
import jax.numpy as jnp
import numpy as np
from jax import lax
from jax.experimental import pallas as pl
from jax.experimental.pallas import tpu as pltpu
from jax.sharding import PartitionSpec as P


EDGE = 0.8
NODE = 0.8 / 7.0

BX, BY, BZ = 8, 16, 128
LOW, HIGH = 3, 4
EXT = LOW + BX + HIGH
VMEM_LIMIT = 16 * 1024 * 1024

VMEM = pl.BlockSpec(memory_space=pltpu.VMEM)
SMEM = pl.BlockSpec(memory_space=pltpu.SMEM)
HBM = pl.BlockSpec(memory_space=pltpu.HBM)


def halo_need():
    size = BX + 9

    def at(need, axis, k):
        return np.roll(need, k, axis)

    out = np.zeros((3, size, size, size), bool)
    out[:, 4 : 4 + BX, 4 : 4 + BX, 4 : 4 + BX] = True
    node = np.zeros((4, size, size, size), bool)
    for a in range(3):
        both = out[a] | at(out[a], a, 1)
        node[0] |= both
        node[a + 1] |= both
    near = node.copy()
    for a in range(3):
        near |= np.roll(node, 1, a + 1) | np.roll(node, -1, a + 1)
    masked = np.stack([near[0] | at(near[0], a, -1) | near[a + 1] | at(near[a + 1], a, -1) for a in range(3)])

    def operand(need):
        face = np.zeros_like(need)
        for a in range(3):
            b, c = (a + 1) % 3, (a + 2) % 3
            face[b] |= need[a] | at(need[a], c, -1)
            face[c] |= need[a] | at(need[a], b, -1)
        edge = need.copy()
        for a in range(3):
            b, c = (a + 1) % 3, (a + 2) % 3
            edge[b] |= face[a] | at(face[a], c, 1)
            edge[c] |= face[a] | at(face[a], b, 1)
        return edge

    second = operand(masked) | out
    first = operand(second)
    return second.any(3).astype(int) + first.any(3).astype(int)


NEED = halo_need()


def plane_need(c, p):
    return NEED[c, p - LOW + 4].max()


def row_counts(c, p):
    need = NEED[c, p - LOW + 4]
    below, above = need[:4], need[4 + BX :]
    return tuple((int((side > 0).sum()), int((side > 1).sum())) for side in (below, above))


OWN = range(LOW, LOW + BX)
BELOW, ABOVE = 0, 1


def y_layout(side):
    at, rows = {}, 0
    for p in OWN:
        for field in range(6):
            count = row_counts(field % 3, p)[side][field // 3]
            at[p, field] = (rows, count)
            rows += count
    rows = -(-rows // 8) * 8
    for p in OWN[::2]:
        at[p, "packed"] = at[p + 1, "packed"] = rows
        rows += 4
    return at, rows


Y_LOW, Y_LOW_ROWS = y_layout(BELOW)
Y_HIGH, Y_HIGH_ROWS = y_layout(ABOVE)
Y_ROWS = -(-max(Y_LOW_ROWS, Y_HIGH_ROWS) // 8) * 8


def x_layout(planes):
    at, rows = {}, 0
    for p in planes:
        for field in range(6):
            if plane_need(field % 3, p) > field // 3:
                at[p, field] = rows
                rows += BY
    for p in planes:
        at[p, "packed"] = rows
        rows += 8
    for p in planes:
        at[p, "edge"] = rows
        rows += 4
    for p in planes:
        for field in range(6):
            for side in (BELOW, ABOVE):
                count = row_counts(field % 3, p)[side][field // 3]
                at[p, field, side] = (rows, count)
                rows += count
    return at, -(-rows // 8) * 8


X_LOW, X_LOW_ROWS = x_layout(range(LOW))
X_HIGH, X_HIGH_ROWS = x_layout(range(LOW + BX, EXT))


def call(body, out_shape, specs, scratch=(), flops=1000000):
    return pl.pallas_call(
        body,
        out_shape=out_shape,
        in_specs=specs,
        out_specs=jax.tree.map(lambda _: VMEM, out_shape),
        scratch_shapes=list(scratch),
        compiler_params=pltpu.CompilerParams(vmem_limit_bytes=VMEM_LIMIT),
        cost_estimate=pl.CostEstimate(flops=flops, bytes_accessed=1000000, transcendentals=0),
    )


def lanes(shape):
    return lax.broadcasted_iota(jnp.int32, shape, 1)


def rotate(v, shift, axis):
    return pltpu.roll(v, shift % v.shape[axis], axis)


def weigh(sigma):
    return jnp.where(sigma > 0.0, EDGE / (4.0 + sigma), 0.0)


def prepare(cond_in, rhs_in, fraction_in, region_in, flags_in, rhs, sigma, first_iter, packed_out, cond, fraction, region, flags, sems):
    copies = [
        pltpu.make_async_copy(source, target, sems.at[i])
        for i, (source, target) in enumerate(
            ((cond_in, cond), (region_in, region), (fraction_in, fraction), (flags_in, flags), (rhs_in, rhs))
        )
    ]
    for copy in copies:
        copy.start()
    for copy in copies:
        copy.wait()
    group = lanes((8, BZ)) // 8
    for x in range(BX):
        where = region[x]
        conductivity = jnp.full((BY, BZ), cond[0], jnp.float32)
        for number in range(1, 8):
            conductivity = jnp.where(where == number, cond[number], conductivity)
        packed = jnp.zeros((8, BZ), jnp.float32)
        for field in range(6):
            if field < 3:
                value = rhs[field, x]
            else:
                c = field - 3
                value = jnp.where(flags[c, x] == 0, conductivity * fraction[c, x], 0.0)
                sigma[c, x] = value
                first_iter[c, x] = weigh(value) * rhs[c, x]
            for tile in range(2):
                slot = field * 2 + tile
                moved = rotate(value[tile * 8 : tile * 8 + 8], LOW + 8 * slot, 1)
                packed = jnp.where(group == slot, moved, packed)
        packed_out[x] = packed


def send_y(ypar, rhs, sigma, first_iter, from_low, from_high, first_out, second_out, packed):
    below = (lanes((8, BZ)) % 8) < LOW
    odd = (lanes((4, BZ)) // 8) % 2
    for x in range(BX):
        packed[x] = jnp.where(below, from_low[x], from_high[x])

    def fill(out, layout, side):
        for p in OWN:
            for c in range(3):
                (at, count), (at_sigma, both) = layout[p, c], layout[p, c + 3]
                inner = 0 if side == ABOVE else BY - both
                outer = both if side == ABOVE else BY - count
                out[at_sigma : at_sigma + both] = sigma[c, p - LOW, inner : inner + both]
                place = at if side == ABOVE else at + count - both
                out[place : place + both] = rhs[c, p - LOW, inner : inner + both]
                place = at + both if side == ABOVE else at
                out[place : place + count - both] = first_iter[c, p - LOW, outer : outer + count - both]
        start = 0 if side == ABOVE else 4
        for p in OWN[::2]:
            value = packed[p - LOW, start : start + 4]
            other = packed[p + 1 - LOW, start : start + 4]
            at = layout[p, "packed"]
            out[at : at + 4] = jnp.where(odd == 1 - side, value, rotate(other, 8 if side == ABOVE else -8, 1))

    @pl.when(ypar[0] == 0)
    def _():
        fill(first_out, Y_LOW, BELOW)
        fill(second_out, Y_HIGH, ABOVE)

    @pl.when(ypar[0] != 0)
    def _():
        fill(second_out, Y_LOW, BELOW)
        fill(first_out, Y_HIGH, ABOVE)


def own_edge(p, y_low, y_high):
    odd = (lanes((4, BZ)) // 8) % 2 == 1
    above = y_high[Y_HIGH[p, "packed"] : Y_HIGH[p, "packed"] + 4]
    below = y_low[Y_LOW[p, "packed"] : Y_LOW[p, "packed"] + 4]
    if (p - LOW) % 2:
        above, below = rotate(above, -8, 1), rotate(below, 8, 1)
    return jnp.where(odd, below, above)


def send_x(ypar, rhs, sigma, first_iter, packed, first, second, up_out, down_out, y_low, y_high):
    even = ypar[0] == 0
    y_high[...] = jnp.where(even, first[1], second[1])
    y_low[...] = jnp.where(even, second[0], first[0])
    for out, layout, planes, step in (
        (up_out, X_LOW, range(LOW), BX),
        (down_out, X_HIGH, range(LOW + BX, EXT), -BX),
    ):
        for p in planes:
            own = p + step
            x = own - LOW
            at = layout[p, "packed"]
            out[at : at + 8] = packed[x]
            at = layout[p, "edge"]
            out[at : at + 4] = own_edge(own, y_low, y_high)
            for c in range(3):
                if plane_need(c, p) == 2:
                    at = layout[p, c]
                    out[at : at + BY] = rhs[c, x]
                    at = layout[p, c + 3]
                    out[at : at + BY] = sigma[c, x]
                elif plane_need(c, p) == 1:
                    at = layout[p, c]
                    out[at : at + BY] = first_iter[c, x]
                for side, source, have in ((BELOW, y_low, Y_LOW), (ABOVE, y_high, Y_HIGH)):
                    (at, count), (at_sigma, both) = layout[p, c, side], layout[p, c + 3, side]
                    (own_at, own_count), (own_sigma, own_both) = have[own, c], have[own, c + 3]

                    def rows(base, size, near, far):
                        return slice(base + near, base + far) if side == ABOVE else slice(base + size - far, base + size - near)

                    if both:
                        out[rows(at_sigma, both, 0, both)] = source[rows(own_sigma, own_both, 0, both)]
                        out[rows(at, count, 0, both)] = source[rows(own_at, own_count, 0, both)]
                    middle = min(max(both, own_both), count)
                    if both < middle:
                        out[rows(at, count, both, middle)] = (
                            weigh(source[rows(own_sigma, own_both, both, middle)])
                            * source[rows(own_at, own_count, both, middle)]
                        )
                    if middle < count:
                        out[rows(at, count, middle, count)] = source[rows(own_at, own_count, middle, count)]


def up_y(v):
    return rotate(v, -1, 0)


def down_y(v):
    return rotate(v, 1, 0)


def up_z(v):
    return rotate(v, -1, 1)


def down_z(v):
    return rotate(v, 1, 1)


def spread(p, main, halo, packed, edge, wide, weight, iterate):
    edge = jnp.concatenate([edge, rotate(edge, -8, 1)], axis=0)
    for field in range(6):
        need = plane_need(field % 3, p)
        if need == 0:
            continue
        target = wide(field, p)
        if need > field // 3:
            target[0:BY, 0:BZ] = main(field)
            rows = halo(field, ABOVE)
            if rows is not None:
                target[BY : BY + rows.shape[0], 0:BZ] = rows
            rows = halo(field, BELOW)
            if rows is not None:
                target[24 - rows.shape[0] : 24, 0:BZ] = rows
        target[0:8, BZ:] = rotate(packed, -(LOW + 16 * field), 1)
        target[8:16, BZ:] = rotate(packed, -(LOW + 16 * field + 8), 1)
        target[16:24, BZ:] = rotate(edge, -(LOW + 16 * field), 1)
    for c in range(3):
        need = plane_need(c, p)
        if need == 0:
            continue
        rhs, sigma, u = wide(c, p), wide(3 + c, p), iterate(c, p)
        if need == 1:
            u[:, 0:BZ] = rhs[:, 0:BZ]
            u[:, BZ:] = weigh(sigma[:, BZ:]) * rhs[:, BZ:]
            continue
        w = weigh(sigma[...])
        weight(c, p)[...] = w
        u[...] = w * rhs[...]
        (low_any, low_both), (high_any, high_both) = row_counts(c, p)
        for start, stop in ((BY + high_both, BY + high_any), (24 - low_any, 24 - low_both)):
            if start < stop:
                u[start:stop, 0:BZ] = rhs[start:stop, 0:BZ]


def faces(u, p):
    u0, u1, u2 = u(0, p)[...], u(1, p)[...], u(2, p)[...]
    f0 = (up_y(u2) - u2) - (up_z(u1) - u1)
    f1 = (up_z(u0) - u0) - (u(2, p + 1)[...] - u2)
    f2 = (u(1, p + 1)[...] - u1) - (up_y(u0) - u0)
    return f0, f1, f2


def curl0(f):
    return (down_z(f[1]) - f[1]) - (down_y(f[2]) - f[2])


def curl1(f, prev):
    return (prev[2] - f[2]) - (down_z(f[0]) - f[0])


def curl2(f, prev):
    return (down_y(f[0]) - f[0]) - (prev[1] - f[1])


def smooth(planes, wide, weight, iterate, second_iter):
    prev = faces(iterate, planes[0] - 1)
    for p in planes:
        f = faces(iterate, p)
        for c, k in enumerate((curl0(f), curl1(f, prev), curl2(f, prev))):
            u = iterate(c, p)[...]
            second_iter(c, p)[...] = u + weight(c, p)[...] * (wide(c, p)[...] - (k + wide(3 + c, p)[...] * u))
        prev = f


def restrict(planes, wide, second_iter, nodal):
    def residual(c, p, k):
        s = wide(3 + c, p)[...]
        return jnp.where(s > 0.0, wide(c, p)[...] - (k + s * second_iter(c, p)[...]), 0.0)

    prev = faces(second_iter, planes[0] - 1)
    before = residual(0, planes[0] - 1, curl0(prev))
    for p in planes:
        f = faces(second_iter, p)
        q0 = residual(0, p, curl0(f))
        q1 = residual(1, p, curl1(f, prev))
        q2 = residual(2, p, curl2(f, prev))
        d1, d2 = down_y(q1), down_z(q2)
        nodal(0, p)[...] = (before - q0) + (d1 - q1) + (d2 - q2)
        nodal(1, p)[...] = (before + q0) * 0.5
        nodal(2, p)[...] = (d1 + q1) * 0.5
        nodal(3, p)[...] = (d2 + q2) * 0.5
        prev, before = f, q0


INNER = {"wide": OWN, "weight": OWN, "iterate": OWN, "second": OWN[1:-1], "nodal": OWN[2:-2]}
USED = {"wide": range(EXT), "weight": range(EXT), "iterate": range(EXT), "second": range(1, EXT - 1), "nodal": range(2, EXT - 2)}
OUTER = {name: [p for p in USED[name] if p not in INNER[name]] for name in USED}
FIELDS = {"wide": 6, "weight": 3, "iterate": 3, "second": 3, "nodal": 4}


def plane_arrays(kind, inner, outer=None):
    at = {p: (inner, i) for i, p in enumerate(INNER[kind])}
    if outer is not None:
        at.update({p: (outer, i) for i, p in enumerate(OUTER[kind])})
    return lambda c, p: at[p][0].at[c, at[p][1]]


def stencil_inner(rhs, sigma, packed, y_low, y_high, *arrays):
    wide, weight, iterate, second_iter, nodal = (plane_arrays(k, ref) for k, ref in zip(FIELDS, arrays))
    for p in OWN:

        def main(field):
            return (rhs if field < 3 else sigma)[field % 3, p - LOW]

        def halo(field, side):
            at, count = (Y_LOW, Y_HIGH)[side][p, field]
            return (y_low, y_high)[side][at : at + count] if count else None

        spread(p, main, halo, packed[p - LOW], own_edge(p, y_low, y_high), wide, weight, iterate)
    smooth(INNER["second"], wide, weight, iterate, second_iter)
    restrict(INNER["nodal"], wide, second_iter, nodal)


def stencil_outer(rhs, sigma, low, high, *arrays):
    inner, out, outer = arrays[:5], arrays[5], arrays[6:]
    wide, weight, iterate, second_iter, nodal = (plane_arrays(k, *refs) for k, refs in zip(FIELDS, zip(inner, outer)))
    for p in OUTER["wide"]:
        ref, layout = (low, X_LOW) if p < LOW else (high, X_HIGH)

        def main(field):
            return ref[layout[p, field] : layout[p, field] + BY]

        def halo(field, side):
            at, count = layout[p, field, side]
            return ref[at : at + count] if count else None

        packed, edge = layout[p, "packed"], layout[p, "edge"]
        spread(p, main, halo, ref[packed : packed + 8], ref[edge : edge + 4], wide, weight, iterate)
    smooth([p for p in OUTER["second"] if p < LOW + 2], wide, weight, iterate, second_iter)
    smooth([p for p in OUTER["second"] if p > LOW + 2], wide, weight, iterate, second_iter)
    restrict([p for p in OUTER["nodal"] if p < LOW + 3], wide, second_iter, nodal)
    restrict([p for p in OUTER["nodal"] if p > LOW + 3], wide, second_iter, nodal)

    def node(c, p):
        b = nodal(c, p)[...]
        near = (nodal(c, p - 1)[...] + nodal(c, p + 1)[...]) + (up_y(b) + down_y(b)) + (up_z(b) + down_z(b))
        return (1.2 * NODE) * b + (NODE * NODE) * near

    n0, n1 = node(0, LOW), node(1, LOW)
    for x in range(BX):
        p = x + LOW
        n0_next, n1_next = node(0, p + 1), node(1, p + 1)
        n2, n3 = node(2, p), node(3, p)
        corrections = (
            (n0_next - n0) + (n1_next + n1) * 0.5,
            (up_y(n0) - n0) + (n2 + up_y(n2)) * 0.5,
            (up_z(n0) - n0) + (n3 + up_z(n3)) * 0.5,
        )
        for c in range(3):
            kept = second_iter(c, p)[0:BY, 0:BZ] + corrections[c][0:BY, 0:BZ]
            out[c, x] = jnp.where(sigma[c, x] > 0.0, kept, 0.96 * rhs[c, x])
        n0, n1 = n0_next, n1_next


def pairs(count):
    return (
        [[i, i + 1] for i in range(0, count, 2)],
        [[i, (i + 1) % count] for i in range(1, count, 2)],
    )


def gather(value, axis, groups):
    return lax.all_gather(value, axis, axis=0, tiled=False, axis_index_groups=groups)


def shift(value, axis, step):
    count = lax.axis_size(axis)
    return lax.ppermute(value, axis, [(i, (i + step) % count) for i in range(count)])


def on_device(rhs, conductivity, fraction, region, flags):
    f32 = functools.partial(jax.ShapeDtypeStruct, dtype=jnp.float32)
    ypar = (lax.axis_index("gy") & 1).astype(jnp.int32).reshape(1)

    block = f32((3, BX, BY, BZ))
    lane_block = f32((BX, 8, BZ))
    rhs, sigma, first_iter, packed = call(
        prepare,
        (block, block, block, lane_block),
        [HBM] * 5,
        scratch=(
            pltpu.SMEM((8,), jnp.float32),
            pltpu.VMEM((3, BX, BY, BZ), jnp.float32),
            pltpu.VMEM((BX, BY, BZ), jnp.int32),
            pltpu.VMEM((3, BX, BY, BZ), jnp.int32),
            pltpu.SemaphoreType.DMA((5,)),
        ),
    )(*(pltpu.with_memory_space_constraint(a, pltpu.HBM) for a in (conductivity, rhs, fraction, region, flags)))

    from_low = shift(packed, "gz", 1)
    from_high = shift(packed, "gz", -1)

    even_y, odd_y = pairs(lax.axis_size("gy"))
    payload = f32((Y_ROWS, BZ))
    to_first, to_second, packed = call(
        send_y, (payload, payload, lane_block), [SMEM] + [VMEM] * 5
    )(ypar, rhs, sigma, first_iter, from_low, from_high)
    first = gather(to_first, "gy", even_y)
    second = gather(to_second, "gy", odd_y)

    up, down, y_low, y_high = call(
        send_x, (f32((X_LOW_ROWS, BZ)), f32((X_HIGH_ROWS, BZ)), payload, payload), [SMEM] + [VMEM] * 6
    )(ypar, rhs, sigma, first_iter, packed, first, second)
    low = shift(up, "gx", 1)
    high = shift(down, "gx", -1)

    inner = call(
        stencil_inner,
        tuple(f32((FIELDS[kind], len(INNER[kind]), 24, 2 * BZ)) for kind in FIELDS),
        [VMEM] * 5,
        flops=20000000,
    )(rhs, sigma, packed, y_low, y_high)
    return call(
        stencil_outer,
        block,
        [VMEM] * 9,
        scratch=[pltpu.VMEM((FIELDS[kind], len(OUTER[kind]), 24, 2 * BZ), jnp.float32) for kind in FIELDS],
    )(rhs, sigma, low, high, *inner)


def solution(mesh):
    return jax.shard_map(
        on_device,
        mesh=mesh,
        in_specs=(
            P(None, "gx", "gy", "gz"),
            P(),
            P(None, "gx", "gy", "gz"),
            P("gx", "gy", "gz"),
            P(None, "gx", "gy", "gz"),
        ),
        out_specs=P(None, "gx", "gy", "gz"),
        check_vma=False,
    )
```

time: 54.1 us -> 53.6 us (level)
  blocking collectives: 30.4 us -> 8.82 us
  starting transfers between devices: 9.48 us -> 26.5 us
  waiting for transfers between devices: 7.43 us -> 11.2 us
    all_gather x4 -> x2, blocking collectives: 30.4 us -> 8.82 us  [gather(): lax.all_gather(value, axis, axis=0, tiled=False, axis_index_groups=groups)]
    ppermute x2 -> x4, starting transfers between devices: 9.48 us -> 26.5 us  [shift(): lax.ppermute(value, axis, [(i, (i + step) % count) for i in range(count)])]
    ppermute x2 -> x4, waiting for transfers between devices: 7.43 us -> 11.2 us  [shift(): lax.ppermute(value, axis, [(i, (i + step) % count) for i in range(count)])]
    pallas_call x4 -> x5, Pallas kernels: 6.61 us -> 6.69 us  [the longest x1 3.54 us: on_device(): call(stencil_outer, block, [VMEM] * 9, scratch=[pltpu.VMEM((FIELDS[kind],...]
  transfers between devices with their start and end apart: 2 -> 4, of which waited for: 1 -> 2; matrix products, arithmetic and copies ran while one was open for 0% -> 0% of each run, Pallas kernels for 0% -> 3%
where the time goes in v4:
time: 53.6 us; the launch traced here: 53.3 us
  starting transfers between devices  26.5 us (49%)
  waiting for transfers between devices  11.2 us (21%)
  blocking collectives  8.82 us (16%)
  Pallas kernels  6.69 us (12%)
    ppermute x4, starting transfers between devices, shift(): lax.ppermute(value, axis, [(i, (i + step) % count) for i in range(count)])  26.5 us
    ppermute x4, waiting for transfers between devices, shift(): lax.ppermute(value, axis, [(i, (i + step) % count) for i in range(count)])  11.2 us
    all_gather x2, blocking collectives, gather(): lax.all_gather(value, axis, axis=0, tiled=False, axis_index_groups=groups)  8.82 us
    pallas_call x1, Pallas kernels, on_device(): call(stencil_outer, block, [VMEM] * 9, scratch=[pltpu.VMEM((FIELDS[kind],...  3.54 us
    pallas_call x1, Pallas kernels, on_device(): call(stencil_inner, tuple((f32((FIELDS[kind], len(INNER[kind]), 24, 2 * B...  1.57 us
    pallas_call x1, Pallas kernels, on_device(): call(prepare, (block, block, block, lane_block), [HBM] * 5, scratch=(pltp...  1.37 us
  transfers between devices with their start and end apart: 4, of which 2 were waited for; matrix products, arithmetic and copies ran while one was open for 0% of the time, Pallas kernels for 3%

profile of v4, /device:TPU:1, one launch (start us, length us, event | category | flops | bytes accessed | tf_op | source)
XLA Modules:
  0.0 53.3 jit_solution(15369568611908855813)
XLA Ops:
  0.0 1.4 %shard_map.55 = (f32[3,8,16,128]{3,2,1,0:T(8,128)S(1)}, f32[3,8,16,128]{3,2,1,0:T(8,128)S(1)}, f32[3,8,16,128]{3,2,1,0:T(8,128)S(1)}, f32[8,8,128]{2,1,0:T(8,128)S(1)}) custom-call(f32[8]{0:T(128)} %cond_in.1, f32[3,8,16,128]{3,2,1,0:T(8,128)} %rhs_in.1, f32[3,8,16,128]{3,2,1,0:T(8,128)} %fraction_in.1, s32[8,16,128]{2,1,0:T(8,128)} %region_in.1, ...), custom_call_target="tpu_custom_call" | custom-call | flops 1000000 | bytes 1000000 | tf_op jit(solution)/shard_map/pallas_call | solution.py:462
  1.4 15.1 %collective-permute-start.1 = (f32[8,8,128]{2,1,0:T(8,128)S(1)}, f32[8,8,128]{2,1,0:T(8,128)S(1)}, u32[]{:S(2)}, u32[]{:S(2)}) collective-permute-start(f32[8,8,128]{2,1,0:T(8,128)S(1)} %get-tuple-element.24), channel_id=1, source_target_pairs={{0,11},{1,0},{2,1},{3,2},{4,3},{5,4},{6,5},{7,6},{8,7},{9,8},{10,9... | collective-permute-start | bytes 98312 | tf_op jit(solution)/shard_map/ppermute | solution.py:453
  16.5 1.9 %collective-permute-start = (f32[8,8,128]{2,1,0:T(8,128)S(1)}, f32[8,8,128]{2,1,0:T(8,128)S(1)}, u32[]{:S(2)}, u32[]{:S(2)}) collective-permute-start(f32[8,8,128]{2,1,0:T(8,128)S(1)} %get-tuple-element.24), channel_id=1, source_target_pairs={{0,1},{1,2},{2,3},{3,4},{4,5},{5,6},{6,7},{7,8},{8,9},{9,10},{10,1... | collective-permute-start | bytes 98312 | tf_op jit(solution)/shard_map/ppermute | solution.py:453
  18.4 0.0 collective-permute-done.1.from_high
  18.4 3.9 %collective-permute-done.from_low = f32[8,8,128]{2,1,0:T(8,128)S(1)} collective-permute-done((f32[8,8,128]{2,1,0:T(8,128)S(1)}, f32[8,8,128]{2,1,0:T(8,128)S(1)}, u32[]{:S(2)}, u32[]{:S(2)}) %collective-permute-start) | collective-permute-done | bytes 32800 | tf_op jit(solution)/shard_map/ppermute | solution.py:453
  22.4 0.1 shard_map.56
  22.5 3.7 %all-gather = f32[336,128]{1,0:T(8,128)S(1)} all-gather(f32[168,128]{1,0:T(8,128)S(1)} %get-tuple-element.26), channel_id=2, replica_groups={{0,12},{24,36},{1,13},{25,37},{2,14},{26,38},{3,15},{27,39},{4,16},{28,..., dimensions={0}, use_global_device_ids=true | all-gather | bytes 258048 | tf_op jit(solution)/shard_map/all_gather | solution.py:448
  26.1 5.1 %all-gather.1 = f32[336,128]{1,0:T(8,128)S(1)} all-gather(f32[168,128]{1,0:T(8,128)S(1)} %get-tuple-element.27), channel_id=3, replica_groups={{12,24},{36,0},{13,25},{37,1},{14,26},{38,2},{15,27},{39,3},{16,28},{40..., dimensions={0}, use_global_device_ids=true | all-gather | bytes 258048 | tf_op jit(solution)/shard_map/all_gather | solution.py:448
  31.3 0.1 shard_map.57
  31.4 7.5 %collective-permute-start.3 = (f32[416,128]{1,0:T(8,128)S(1)}, f32[416,128]{1,0:T(8,128)S(1)}, u32[]{:S(2)}, u32[]{:S(2)}) collective-permute-start(f32[416,128]{1,0:T(8,128)S(1)} %get-tuple-element.29), channel_id=1, source_target_pairs={{0,720},{48,0},{96,48},{144,96},{192,144},{240,192},{288,240},{336... | collective-permute-start | bytes 638984 | tf_op jit(solution)/shard_map/ppermute | solution.py:453
  39.0 1.9 %collective-permute-start.2 = (f32[336,128]{1,0:T(8,128)S(1)}, f32[336,128]{1,0:T(8,128)S(1)}, u32[]{:S(2)}, u32[]{:S(2)}) collective-permute-start(f32[336,128]{1,0:T(8,128)S(1)} %get-tuple-element.28), channel_id=1, source_target_pairs={{0,48},{48,96},{96,144},{144,192},{192,240},{240,288},{288,336},{3... | collective-permute-start | bytes 516104 | tf_op jit(solution)/shard_map/ppermute | solution.py:453
  40.9 1.6 %shard_map.58 = (f32[6,8,24,256]{3,2,1,0:T(8,128)S(1)}, f32[3,8,24,256]{3,2,1,0:T(8,128)S(1)}, f32[3,8,24,256]{3,2,1,0:T(8,128)S(1)}, f32[3,6,24,256]{3,2,1,0:T(8,128)S(1)}, f32[4,4,24,256]{3,2,1,0:T(8,128)S(1)}) custom-call(f32[3,8,16,128]{3,2,1,0:T(8,128)S(1)} %get-tuple-element.21.rhs, f32[3,8,16,128]{3,2,1,0:T(8,128)S(1)} %get-tuple-element.22.sigma, ...), custom_call_target="tpu_custom_call" | custom-call | flops 20000000 | bytes 1000000 | tf_op jit(solution)/shard_map/pallas_call | solution.py:492
  42.5 7.3 %collective-permute-done.2.low = f32[336,128]{1,0:T(8,128)S(1)} collective-permute-done((f32[336,128]{1,0:T(8,128)S(1)}, f32[336,128]{1,0:T(8,128)S(1)}, u32[]{:S(2)}, u32[]{:S(2)}) %collective-permute-start.2) | collective-permute-done | bytes 172064 | tf_op jit(solution)/shard_map/ppermute | solution.py:453
  49.8 0.0 collective-permute-done.3.high
  49.8 3.5 %shard_map.59 = f32[3,8,16,128]{3,2,1,0:T(8,128)} custom-call(f32[3,8,16,128]{3,2,1,0:T(8,128)S(1)} %get-tuple-element.21.rhs, f32[3,8,16,128]{3,2,1,0:T(8,128)S(1)} %get-tuple-element.22.sigma, f32[336,128]{1,0:T(8,128)S(1)} %collective-permute-done.2.low, f32[416,128]{1,0:T(8,128)S(1)} %collective-permute-done.3.high, ...), custom_call_target="tpu_custom_call" | custom-call | flops 1000000 | bytes 1000000 | tf_op jit(solution)/shard_map/pallas_call | solution.py:498
Async XLA Ops:
  1.4 17.1 %collective-permute-start.1 = (f32[8,8,128]{2,1,0:T(8,128)S(1)}, f32[8,8,128]{2,1,0:T(8,128)S(1)}, u32[]{:S(2)}, u32[]{:S(2)}) collective-permute-start(f32[8,8,128]{2,1,0:T(8,128)S(1)} %get-tuple-element.24), channel_id=1, source_target_pairs={{0,11},{1,0},{2,1},{3,2},{4,3},{5,4},{6,5},{7,6},{8,7},{9,8},{10,9... | collective-permute-start | bytes 98312 | tf_op jit(solution)/shard_map/ppermute | solution.py:453
  16.5 5.9 %collective-permute-start = (f32[8,8,128]{2,1,0:T(8,128)S(1)}, f32[8,8,128]{2,1,0:T(8,128)S(1)}, u32[]{:S(2)}, u32[]{:S(2)}) collective-permute-start(f32[8,8,128]{2,1,0:T(8,128)S(1)} %get-tuple-element.24), channel_id=1, source_target_pairs={{0,1},{1,2},{2,3},{3,4},{4,5},{5,6},{6,7},{7,8},{8,9},{9,10},{10,1... | collective-permute-start | bytes 98312 | tf_op jit(solution)/shard_map/ppermute | solution.py:453
  31.4 18.4 %collective-permute-start.3 = (f32[416,128]{1,0:T(8,128)S(1)}, f32[416,128]{1,0:T(8,128)S(1)}, u32[]{:S(2)}, u32[]{:S(2)}) collective-permute-start(f32[416,128]{1,0:T(8,128)S(1)} %get-tuple-element.29), channel_id=1, source_target_pairs={{0,720},{48,0},{96,48},{144,96},{192,144},{240,192},{288,240},{336... | collective-permute-start | bytes 638984 | tf_op jit(solution)/shard_map/ppermute | solution.py:453
  39.0 10.8 %collective-permute-start.2 = (f32[336,128]{1,0:T(8,128)S(1)}, f32[336,128]{1,0:T(8,128)S(1)}, u32[]{:S(2)}, u32[]{:S(2)}) collective-permute-start(f32[336,128]{1,0:T(8,128)S(1)} %get-tuple-element.28), channel_id=1, source_target_pairs={{0,48},{48,96},{96,144},{144,192},{192,240},{240,288},{288,336},{3... | collective-permute-start | bytes 516104 | tf_op jit(solution)/shard_map/ppermute | solution.py:453

commit v5 on v4

--- a/solution.py
+++ b/solution.py
@@ -337,40 +337,78 @@
     return (down_y(f[0]) - f[0]) - (prev[1] - f[1])
 
 
-def smooth(planes, wide, weight, iterate, second_iter):
-    prev = faces(iterate, planes[0] - 1)
+def update(c, p, k, wide, weight, iterate):
+    u = iterate(c, p)[...]
+    return u + weight(c, p)[...] * (wide(c, p)[...] - (k + wide(3 + c, p)[...] * u))
+
+
+def smooth(planes, prev, wide, weight, iterate, second_iter):
     for p in planes:
         f = faces(iterate, p)
         for c, k in enumerate((curl0(f), curl1(f, prev), curl2(f, prev))):
-            u = iterate(c, p)[...]
-            second_iter(c, p)[...] = u + weight(c, p)[...] * (wide(c, p)[...] - (k + wide(3 + c, p)[...] * u))
+            second_iter(c, p)[...] = update(c, p, k, wide, weight, iterate)
         prev = f
-
-
-def restrict(planes, wide, second_iter, nodal):
-    def residual(c, p, k):
-        s = wide(3 + c, p)[...]
-        return jnp.where(s > 0.0, wide(c, p)[...] - (k + s * second_iter(c, p)[...]), 0.0)
-
-    prev = faces(second_iter, planes[0] - 1)
-    before = residual(0, planes[0] - 1, curl0(prev))
+    return prev
+
+
+def defect(c, p, k, wide, second_iter):
+    return wide(c, p)[...] - (k + wide(3 + c, p)[...] * second_iter(c, p)[...])
+
+
+def kept(c, p, value, wide):
+    return jnp.where(wide(3 + c, p)[...] > 0.0, value, 0.0)
+
+
+def gather_nodes(p, before, q0, q1, q2, nodal):
+    d1, d2 = down_y(q1), down_z(q2)
+    nodal(0, p)[...] = (before - q0) + (d1 - q1) + (d2 - q2)
+    nodal(1, p)[...] = (before + q0) * 0.5
+    nodal(2, p)[...] = (d1 + q1) * 0.5
+    nodal(3, p)[...] = (d2 + q2) * 0.5
+
+
+def restrict(planes, prev, before, wide, second_iter, nodal):
     for p in planes:
         f = faces(second_iter, p)
-        q0 = residual(0, p, curl0(f))
-        q1 = residual(1, p, curl1(f, prev))
-        q2 = residual(2, p, curl2(f, prev))
-        d1, d2 = down_y(q1), down_z(q2)
-        nodal(0, p)[...] = (before - q0) + (d1 - q1) + (d2 - q2)
-        nodal(1, p)[...] = (before + q0) * 0.5
-        nodal(2, p)[...] = (d1 + q1) * 0.5
-        nodal(3, p)[...] = (d2 + q2) * 0.5
-        prev, before = f, q0
+        q = [
+            kept(c, p, defect(c, p, k, wide, second_iter), wide)
+            for c, k in enumerate((curl0(f), curl1(f, prev), curl2(f, prev)))
+        ]
+        gather_nodes(p, before, *q, nodal)
+        prev, before = f, q[0]
+    return prev, before
+
+
+def beside(c, p, nodal):
+    b = nodal(c, p)[...]
+    return (1.2 * NODE) * b + (NODE * NODE) * ((up_y(b) + down_y(b)) + (up_z(b) + down_z(b)))
+
+
+def finish(p, n0, n0_next, n1, n1_next, n2, n3, second_iter, rhs, sigma):
+    corrections = (
+        (n0_next - n0) + (n1_next + n1) * 0.5,
+        (up_y(n0) - n0) + (n2 + up_y(n2)) * 0.5,
+        (up_z(n0) - n0) + (n3 + up_z(n3)) * 0.5,
+    )
+    return [
+        jnp.where(
+            sigma[c, p - LOW] > 0.0,
+            second_iter(c, p)[0:BY, 0:BZ] + corrections[c][0:BY, 0:BZ],
+            0.96 * rhs[c, p - LOW],
+        )
+        for c in range(3)
+    ]
 
 
 INNER = {"wide": OWN, "weight": OWN, "iterate": OWN, "second": OWN[1:-1], "nodal": OWN[2:-2]}
 USED = {"wide": range(EXT), "weight": range(EXT), "iterate": range(EXT), "second": range(1, EXT - 1), "nodal": range(2, EXT - 2)}
 OUTER = {name: [p for p in USED[name] if p not in INNER[name]] for name in USED}
-FIELDS = {"wide": 6, "weight": 3, "iterate": 3, "second": 3, "nodal": 4}
+INNER |= {"second_part": OWN[:1], "second_carry": OWN[-2:-1], "nodal_part": OWN[1:2], "nodal_carry": OWN[-3:-2], "beside": OWN[2:-2]}
+FIELDS = {
+    "wide": 6, "weight": 3, "iterate": 3, "second": 3, "nodal": 4,
+    "second_part": 3, "second_carry": 2, "nodal_part": 3, "nodal_carry": 3, "beside": 4,
+}
+MIDDLE = OWN[3]
 
 
 def plane_arrays(kind, inner, outer=None):
@@ -380,8 +418,10 @@
     return lambda c, p: at[p][0].at[c, at[p][1]]
 
 
-def stencil_inner(rhs, sigma, packed, y_low, y_high, *arrays):
-    wide, weight, iterate, second_iter, nodal = (plane_arrays(k, ref) for k, ref in zip(FIELDS, arrays))
+def stencil_inner(rhs, sigma, packed, y_low, y_high, middle, *arrays):
+    wide, weight, iterate, second_iter, nodal, second_part, second_carry, nodal_part, nodal_carry, near = (
+        plane_arrays(kind, ref) for kind, ref in zip(FIELDS, arrays)
+    )
     for p in OWN:
 
         def main(field):
@@ -392,13 +432,47 @@
             return (y_low, y_high)[side][at : at + count] if count else None
 
         spread(p, main, halo, packed[p - LOW], own_edge(p, y_low, y_high), wide, weight, iterate)
-    smooth(INNER["second"], wide, weight, iterate, second_iter)
-    restrict(INNER["nodal"], wide, second_iter, nodal)
-
-
-def stencil_outer(rhs, sigma, low, high, *arrays):
-    inner, out, outer = arrays[:5], arrays[5], arrays[6:]
+
+    p = OWN[0]
+    prev = f = faces(iterate, p)
+    k = (curl0(f), -f[2] - (down_z(f[0]) - f[0]), (down_y(f[0]) - f[0]) + f[1])
+    for c in range(3):
+        second_part(c, p)[...] = update(c, p, k[c], wide, weight, iterate)
+    prev = smooth(INNER["second"], prev, wide, weight, iterate, second_iter)
+    for i in range(2):
+        second_carry(i, INNER["second"][-1])[...] = prev[1 + i]
+
+    p = OWN[1]
+    prev = f = faces(second_iter, p)
+    before = kept(0, p, defect(0, p, curl0(f), wide, second_iter), wide)
+    nodal_part(0, p)[...] = before
+    nodal_part(1, p)[...] = defect(1, p, -f[2] - (down_z(f[0]) - f[0]), wide, second_iter)
+    nodal_part(2, p)[...] = defect(2, p, (down_y(f[0]) - f[0]) + f[1], wide, second_iter)
+    prev, before = restrict(INNER["nodal"], prev, before, wide, second_iter, nodal)
+    for i, value in enumerate((prev[1], prev[2], before)):
+        nodal_carry(i, INNER["nodal"][-1])[...] = value
+
+    for p in INNER["beside"]:
+        for c in range(4):
+            near(c, p)[...] = beside(c, p, nodal)
+
+    def node(c, p):
+        return near(c, p)[...] + (NODE * NODE) * (nodal(c, p - 1)[...] + nodal(c, p + 1)[...])
+
+    p = MIDDLE
+    planes = finish(
+        p, node(0, p), node(0, p + 1), node(1, p), node(1, p + 1), node(2, p), node(3, p), second_iter, rhs, sigma
+    )
+    for c in range(3):
+        middle[c] = planes[c]
+
+
+def stencil_outer(rhs, sigma, low, high, middle, *arrays):
+    inner, out, outer = arrays[: len(FIELDS)], arrays[len(FIELDS)], arrays[len(FIELDS) + 1 :]
     wide, weight, iterate, second_iter, nodal = (plane_arrays(k, *refs) for k, refs in zip(FIELDS, zip(inner, outer)))
+    second_part, second_carry, nodal_part, nodal_carry, near = (
+        plane_arrays(kind, ref) for kind, ref in list(zip(FIELDS, inner))[5:]
+    )
     for p in OUTER["wide"]:
         ref, layout = (low, X_LOW) if p < LOW else (high, X_HIGH)
 
@@ -411,29 +485,38 @@
 
         packed, edge = layout[p, "packed"], layout[p, "edge"]
         spread(p, main, halo, ref[packed : packed + 8], ref[edge : edge + 4], wide, weight, iterate)
-    smooth([p for p in OUTER["second"] if p < LOW + 2], wide, weight, iterate, second_iter)
-    smooth([p for p in OUTER["second"] if p > LOW + 2], wide, weight, iterate, second_iter)
-    restrict([p for p in OUTER["nodal"] if p < LOW + 3], wide, second_iter, nodal)
-    restrict([p for p in OUTER["nodal"] if p > LOW + 3], wide, second_iter, nodal)
+
+    first, last = INNER["second"][0] - 1, INNER["second"][-1]
+    prev = smooth(range(1, first), faces(iterate, 0), wide, weight, iterate, second_iter)
+    second_iter(0, first)[...] = second_part(0, first)[...]
+    second_iter(1, first)[...] = second_part(1, first)[...] - weight(1, first)[...] * prev[2]
+    second_iter(2, first)[...] = second_part(2, first)[...] + weight(2, first)[...] * prev[1]
+    prev = (None, second_carry(0, last)[...], second_carry(1, last)[...])
+    smooth(range(last + 1, EXT - 1), prev, wide, weight, iterate, second_iter)
+
+    first, last = INNER["nodal"][0] - 1, INNER["nodal"][-1]
+    prev = faces(second_iter, 1)
+    before = kept(0, 1, defect(0, 1, curl0(prev), wide, second_iter), wide)
+    prev, before = restrict(range(2, first), prev, before, wide, second_iter, nodal)
+    q1 = kept(1, first, nodal_part(1, first)[...] - prev[2], wide)
+    q2 = kept(2, first, nodal_part(2, first)[...] + prev[1], wide)
+    gather_nodes(first, before, nodal_part(0, first)[...], q1, q2, nodal)
+    prev = (None, nodal_carry(0, last)[...], nodal_carry(1, last)[...])
+    restrict(range(last + 1, EXT - 2), prev, nodal_carry(2, last)[...], wide, second_iter, nodal)
 
     def node(c, p):
-        b = nodal(c, p)[...]
-        near = (nodal(c, p - 1)[...] + nodal(c, p + 1)[...]) + (up_y(b) + down_y(b)) + (up_z(b) + down_z(b))
-        return (1.2 * NODE) * b + (NODE * NODE) * near
+        own = near(c, p)[...] if p in INNER["beside"] else beside(c, p, nodal)
+        return own + (NODE * NODE) * (nodal(c, p - 1)[...] + nodal(c, p + 1)[...])
 
     n0, n1 = node(0, LOW), node(1, LOW)
-    for x in range(BX):
-        p = x + LOW
+    for p in OWN:
         n0_next, n1_next = node(0, p + 1), node(1, p + 1)
-        n2, n3 = node(2, p), node(3, p)
-        corrections = (
-            (n0_next - n0) + (n1_next + n1) * 0.5,
-            (up_y(n0) - n0) + (n2 + up_y(n2)) * 0.5,
-            (up_z(n0) - n0) + (n3 + up_z(n3)) * 0.5,
-        )
+        if p == MIDDLE:
+            planes = [middle[c] for c in range(3)]
+        else:
+            planes = finish(p, n0, n0_next, n1, n1_next, node(2, p), node(3, p), second_iter, rhs, sigma)
         for c in range(3):
-            kept = second_iter(c, p)[0:BY, 0:BZ] + corrections[c][0:BY, 0:BZ]
-            out[c, x] = jnp.where(sigma[c, x] > 0.0, kept, 0.96 * rhs[c, x])
+            out[c, p - LOW] = planes[c]
         n0, n1 = n0_next, n1_next
 
 
@@ -491,15 +574,15 @@
 
     inner = call(
         stencil_inner,
-        tuple(f32((FIELDS[kind], len(INNER[kind]), 24, 2 * BZ)) for kind in FIELDS),
+        (f32((3, BY, BZ)), *(f32((FIELDS[kind], len(INNER[kind]), 24, 2 * BZ)) for kind in FIELDS)),
         [VMEM] * 5,
         flops=20000000,
     )(rhs, sigma, packed, y_low, y_high)
     return call(
         stencil_outer,
         block,
-        [VMEM] * 9,
-        scratch=[pltpu.VMEM((FIELDS[kind], len(OUTER[kind]), 24, 2 * BZ), jnp.float32) for kind in FIELDS],
+        [VMEM] * (5 + len(FIELDS)),
+        scratch=[pltpu.VMEM((FIELDS[kind], len(OUTER[kind]), 24, 2 * BZ), jnp.float32) for kind in OUTER],
     )(rhs, sigma, low, high, *inner)
 
 

time: 53.6 us -> 52.9 us (0.987)
  transfers between devices with their start and end apart: 4 -> 4, of which waited for: 2 -> 2; matrix products, arithmetic and copies ran while one was open for 0% -> 0% of each run, Pallas kernels for 3% -> 4%
where the time goes in v5:
time: 52.9 us; the launch traced here: 52.6 us
  starting transfers between devices  26.5 us (50%)
  waiting for transfers between devices  10.9 us (21%)
  blocking collectives  8.82 us (17%)
  Pallas kernels  6.35 us (12%)
    ppermute x4, starting transfers between devices, shift(): lax.ppermute(value, axis, [(i, (i + step) % count) for i in range(count)])  26.5 us
    ppermute x4, waiting for transfers between devices, shift(): lax.ppermute(value, axis, [(i, (i + step) % count) for i in range(count)])  10.9 us
    all_gather x2, blocking collectives, gather(): lax.all_gather(value, axis, axis=0, tiled=False, axis_index_groups=groups)  8.82 us
    pallas_call x1, Pallas kernels, on_device(): call(stencil_outer, block, [VMEM] * (5 + len(FIELDS)), scratch=[pltpu.VME...  2.8 us
    pallas_call x1, Pallas kernels, on_device(): call(stencil_inner, (f32((3, BY, BZ)), *(f32((FIELDS[kind], len(INNER[kin...  1.96 us
    pallas_call x1, Pallas kernels, on_device(): call(prepare, (block, block, block, lane_block), [HBM] * 5, scratch=(pltp...  1.37 us
  transfers between devices with their start and end apart: 4, of which 2 were waited for; matrix products, arithmetic and copies ran while one was open for 0% of the time, Pallas kernels for 4%

profile of v5, /device:TPU:1, one launch (start us, length us, event | category | flops | bytes accessed | tf_op | source)
XLA Modules:
  0.0 52.6 jit_solution(3574155180178114240)
XLA Ops:
  0.0 1.4 %shard_map.55 = (f32[3,8,16,128]{3,2,1,0:T(8,128)S(1)}, f32[3,8,16,128]{3,2,1,0:T(8,128)S(1)}, f32[3,8,16,128]{3,2,1,0:T(8,128)S(1)}, f32[8,8,128]{2,1,0:T(8,128)S(1)}) custom-call(f32[8]{0:T(128)} %cond_in.1, f32[3,8,16,128]{3,2,1,0:T(8,128)} %rhs_in.1, f32[3,8,16,128]{3,2,1,0:T(8,128)} %fraction_in.1, s32[8,16,128]{2,1,0:T(8,128)} %region_in.1, ...), custom_call_target="tpu_custom_call" | custom-call | flops 1000000 | bytes 1000000 | tf_op jit(solution)/shard_map/pallas_call | solution.py:545
  1.4 15.1 %collective-permute-start.1 = (f32[8,8,128]{2,1,0:T(8,128)S(1)}, f32[8,8,128]{2,1,0:T(8,128)S(1)}, u32[]{:S(2)}, u32[]{:S(2)}) collective-permute-start(f32[8,8,128]{2,1,0:T(8,128)S(1)} %get-tuple-element.30), channel_id=1, source_target_pairs={{0,11},{1,0},{2,1},{3,2},{4,3},{5,4},{6,5},{7,6},{8,7},{9,8},{10,9... | collective-permute-start | bytes 98312 | tf_op jit(solution)/shard_map/ppermute | solution.py:536
  16.5 1.9 %collective-permute-start = (f32[8,8,128]{2,1,0:T(8,128)S(1)}, f32[8,8,128]{2,1,0:T(8,128)S(1)}, u32[]{:S(2)}, u32[]{:S(2)}) collective-permute-start(f32[8,8,128]{2,1,0:T(8,128)S(1)} %get-tuple-element.30), channel_id=1, source_target_pairs={{0,1},{1,2},{2,3},{3,4},{4,5},{5,6},{6,7},{7,8},{8,9},{9,10},{10,1... | collective-permute-start | bytes 98312 | tf_op jit(solution)/shard_map/ppermute | solution.py:536
  18.4 0.0 collective-permute-done.1.from_high
  18.4 3.9 %collective-permute-done.from_low = f32[8,8,128]{2,1,0:T(8,128)S(1)} collective-permute-done((f32[8,8,128]{2,1,0:T(8,128)S(1)}, f32[8,8,128]{2,1,0:T(8,128)S(1)}, u32[]{:S(2)}, u32[]{:S(2)}) %collective-permute-start) | collective-permute-done | bytes 32800 | tf_op jit(solution)/shard_map/ppermute | solution.py:536
  22.4 0.1 shard_map.56
  22.5 3.7 %all-gather = f32[336,128]{1,0:T(8,128)S(1)} all-gather(f32[168,128]{1,0:T(8,128)S(1)} %get-tuple-element.32), channel_id=2, replica_groups={{0,12},{24,36},{1,13},{25,37},{2,14},{26,38},{3,15},{27,39},{4,16},{28,..., dimensions={0}, use_global_device_ids=true | all-gather | bytes 258048 | tf_op jit(solution)/shard_map/all_gather | solution.py:531
  26.1 5.1 %all-gather.1 = f32[336,128]{1,0:T(8,128)S(1)} all-gather(f32[168,128]{1,0:T(8,128)S(1)} %get-tuple-element.33), channel_id=3, replica_groups={{12,24},{36,0},{13,25},{37,1},{14,26},{38,2},{15,27},{39,3},{16,28},{40..., dimensions={0}, use_global_device_ids=true | all-gather | bytes 258048 | tf_op jit(solution)/shard_map/all_gather | solution.py:531
  31.3 0.1 shard_map.57
  31.4 7.5 %collective-permute-start.3 = (f32[416,128]{1,0:T(8,128)S(1)}, f32[416,128]{1,0:T(8,128)S(1)}, u32[]{:S(2)}, u32[]{:S(2)}) collective-permute-start(f32[416,128]{1,0:T(8,128)S(1)} %get-tuple-element.35), channel_id=1, source_target_pairs={{0,720},{48,0},{96,48},{144,96},{192,144},{240,192},{288,240},{336... | collective-permute-start | bytes 638984 | tf_op jit(solution)/shard_map/ppermute | solution.py:536
  39.0 1.9 %collective-permute-start.2 = (f32[336,128]{1,0:T(8,128)S(1)}, f32[336,128]{1,0:T(8,128)S(1)}, u32[]{:S(2)}, u32[]{:S(2)}) collective-permute-start(f32[336,128]{1,0:T(8,128)S(1)} %get-tuple-element.34), channel_id=1, source_target_pairs={{0,48},{48,96},{96,144},{144,192},{192,240},{240,288},{288,336},{3... | collective-permute-start | bytes 516104 | tf_op jit(solution)/shard_map/ppermute | solution.py:536
  40.9 2.0 %shard_map.58 = (f32[3,16,128]{2,1,0:T(8,128)S(1)}, f32[6,8,24,256]{3,2,1,0:T(8,128)S(1)}, f32[3,8,24,256]{3,2,1,0:T(8,128)S(1)}, f32[3,8,24,256]{3,2,1,0:T(8,12...) custom-call(f32[3,8,16,128]{3,2,1,0:T(8,128)S(1)} %get-tuple-element, ...), custom_call_target="tpu_custom_call" | custom-call | flops 20000000 | bytes 1000000 | tf_op jit(solution)/shard_map/pallas_call | solution.py:575
  42.9 6.9 %collective-permute-done.2.low = f32[336,128]{1,0:T(8,128)S(1)} collective-permute-done((f32[336,128]{1,0:T(8,128)S(1)}, f32[336,128]{1,0:T(8,128)S(1)}, u32[]{:S(2)}, u32[]{:S(2)}) %collective-permute-start.2) | collective-permute-done | bytes 172064 | tf_op jit(solution)/shard_map/ppermute | solution.py:536
  49.8 0.0 collective-permute-done.3.high
  49.8 2.8 %shard_map.59 = f32[3,8,16,128]{3,2,1,0:T(8,128)} custom-call(f32[3,8,16,128]{3,2,1,0:T(8,128)S(1)} %get-tuple-element.27.rhs, f32[3,8,16,128]{3,2,1,0:T(8,128)S(1)} %get-tuple-element.28.sigma, f32[336,128]{1,0:T(8,128)S(1)} %collective-permute-done.2.low, f32[416,128]{1,0:T(8,128)S(1)} %collective-permute-done.3.high, ...), custom_call_target="tpu_custom_call" | custom-call | flops 1000000 | bytes 1000000 | tf_op jit(solution)/shard_map/pallas_call | solution.py:581
Async XLA Ops:
  1.4 17.1 %collective-permute-start.1 = (f32[8,8,128]{2,1,0:T(8,128)S(1)}, f32[8,8,128]{2,1,0:T(8,128)S(1)}, u32[]{:S(2)}, u32[]{:S(2)}) collective-permute-start(f32[8,8,128]{2,1,0:T(8,128)S(1)} %get-tuple-element.30), channel_id=1, source_target_pairs={{0,11},{1,0},{2,1},{3,2},{4,3},{5,4},{6,5},{7,6},{8,7},{9,8},{10,9... | collective-permute-start | bytes 98312 | tf_op jit(solution)/shard_map/ppermute | solution.py:536
  16.5 5.9 %collective-permute-start = (f32[8,8,128]{2,1,0:T(8,128)S(1)}, f32[8,8,128]{2,1,0:T(8,128)S(1)}, u32[]{:S(2)}, u32[]{:S(2)}) collective-permute-start(f32[8,8,128]{2,1,0:T(8,128)S(1)} %get-tuple-element.30), channel_id=1, source_target_pairs={{0,1},{1,2},{2,3},{3,4},{4,5},{5,6},{6,7},{7,8},{8,9},{9,10},{10,1... | collective-permute-start | bytes 98312 | tf_op jit(solution)/shard_map/ppermute | solution.py:536
  31.4 18.4 %collective-permute-start.3 = (f32[416,128]{1,0:T(8,128)S(1)}, f32[416,128]{1,0:T(8,128)S(1)}, u32[]{:S(2)}, u32[]{:S(2)}) collective-permute-start(f32[416,128]{1,0:T(8,128)S(1)} %get-tuple-element.35), channel_id=1, source_target_pairs={{0,720},{48,0},{96,48},{144,96},{192,144},{240,192},{288,240},{336... | collective-permute-start | bytes 638984 | tf_op jit(solution)/shard_map/ppermute | solution.py:536
  39.0 10.8 %collective-permute-start.2 = (f32[336,128]{1,0:T(8,128)S(1)}, f32[336,128]{1,0:T(8,128)S(1)}, u32[]{:S(2)}, u32[]{:S(2)}) collective-permute-start(f32[336,128]{1,0:T(8,128)S(1)} %get-tuple-element.34), channel_id=1, source_target_pairs={{0,48},{48,96},{96,144},{144,192},{192,240},{240,288},{288,336},{3... | collective-permute-start | bytes 516104 | tf_op jit(solution)/shard_map/ppermute | solution.py:536

commit v6 on v5

--- a/solution.py
+++ b/solution.py
@@ -102,17 +102,19 @@
                 at[p, field] = rows
                 rows += BY
     for p in planes:
-        at[p, "packed"] = rows
-        rows += 8
-    for p in planes:
-        at[p, "edge"] = rows
-        rows += 4
-    for p in planes:
         for field in range(6):
             for side in (BELOW, ABOVE):
                 count = row_counts(field % 3, p)[side][field // 3]
                 at[p, field, side] = (rows, count)
                 rows += count
+    rows = -(-rows // 4) * 4
+    for p in planes:
+        at[p, "edge"] = rows
+        rows += 4
+    rows = -(-rows // 8) * 8
+    for p in planes:
+        at[p, "packed"] = rows
+        rows += 8
     return at, -(-rows // 8) * 8
 
 
@@ -177,11 +179,12 @@
         packed_out[x] = packed
 
 
-def send_y(ypar, rhs, sigma, first_iter, from_low, from_high, first_out, second_out, packed):
+def send_y(ypar, zpar, rhs, sigma, first_iter, from_even, from_odd, first_out, second_out, packed):
     below = (lanes((8, BZ)) % 8) < LOW
     odd = (lanes((4, BZ)) // 8) % 2
+    below = below == (zpar[0] == 0)
     for x in range(BX):
-        packed[x] = jnp.where(below, from_low[x], from_high[x])
+        packed[x] = jnp.where(below, jnp.where(zpar[0] == 0, from_odd[0, x], from_odd[1, x]), from_even[x])
 
     def fill(out, layout, side):
         for p in OWN:
@@ -221,6 +224,15 @@
     return jnp.where(odd, below, above)
 
 
+def first_lanes(p, value):
+    fields = [c for c in range(3) if plane_need(c, p) == 1]
+    if not fields:
+        return value
+    field = lanes(value.shape) // 16
+    chosen = (field >= fields[0]) & (field <= fields[-1])
+    return jnp.where(chosen, weigh(rotate(value, -48, 1)) * value, value)
+
+
 def send_x(ypar, rhs, sigma, first_iter, packed, first, second, up_out, down_out, y_low, y_high):
     even = ypar[0] == 0
     y_high[...] = jnp.where(even, first[1], second[1])
@@ -233,9 +245,9 @@
             own = p + step
             x = own - LOW
             at = layout[p, "packed"]
-            out[at : at + 8] = packed[x]
+            out[at : at + 8] = first_lanes(p, packed[x])
             at = layout[p, "edge"]
-            out[at : at + 4] = own_edge(own, y_low, y_high)
+            out[at : at + 4] = first_lanes(p, own_edge(own, y_low, y_high))
             for c in range(3):
                 if plane_need(c, p) == 2:
                     at = layout[p, c]
@@ -281,40 +293,39 @@
     return rotate(v, 1, 1)
 
 
-def spread(p, main, halo, packed, edge, wide, weight, iterate):
+def spread(p, main, tile, packed, edge, wide, weight, iterate):
     edge = jnp.concatenate([edge, rotate(edge, -8, 1)], axis=0)
-    for field in range(6):
-        need = plane_need(field % 3, p)
-        if need == 0:
-            continue
-        target = wide(field, p)
-        if need > field // 3:
-            target[0:BY, 0:BZ] = main(field)
-            rows = halo(field, ABOVE)
-            if rows is not None:
-                target[BY : BY + rows.shape[0], 0:BZ] = rows
-            rows = halo(field, BELOW)
-            if rows is not None:
-                target[24 - rows.shape[0] : 24, 0:BZ] = rows
-        target[0:8, BZ:] = rotate(packed, -(LOW + 16 * field), 1)
-        target[8:16, BZ:] = rotate(packed, -(LOW + 16 * field + 8), 1)
-        target[16:24, BZ:] = rotate(edge, -(LOW + 16 * field), 1)
+    row = lax.broadcasted_iota(jnp.int32, (8, BZ), 0)
+
+    def parts(field):
+        at = LOW + 16 * field
+        return (
+            (slice(0, BY), slice(0, BZ), main(field)),
+            (slice(BY, 24), slice(0, BZ), tile(field)),
+            (slice(0, 8), slice(BZ, None), rotate(packed, -at, 1)),
+            (slice(8, BY), slice(BZ, None), rotate(packed, -(at + 8), 1)),
+            (slice(BY, 24), slice(BZ, None), rotate(edge, -at, 1)),
+        )
+
     for c in range(3):
         need = plane_need(c, p)
         if need == 0:
             continue
-        rhs, sigma, u = wide(c, p), wide(3 + c, p), iterate(c, p)
         if need == 1:
-            u[:, 0:BZ] = rhs[:, 0:BZ]
-            u[:, BZ:] = weigh(sigma[:, BZ:]) * rhs[:, BZ:]
+            for rows, columns, value in parts(c):
+                iterate(c, p)[rows, columns] = value
             continue
-        w = weigh(sigma[...])
-        weight(c, p)[...] = w
-        u[...] = w * rhs[...]
         (low_any, low_both), (high_any, high_both) = row_counts(c, p)
-        for start, stop in ((BY + high_both, BY + high_any), (24 - low_any, 24 - low_both)):
-            if start < stop:
-                u[start:stop, 0:BZ] = rhs[start:stop, 0:BZ]
+        single = ((row >= high_both) & (row < high_any)) | ((row >= 8 - low_any) & (row < 8 - low_both))
+        for i, ((rows, columns, rhs), (_, _, sigma)) in enumerate(zip(parts(c), parts(3 + c))):
+            w = weigh(sigma)
+            u = w * rhs
+            if i == 1 and (high_any > high_both or low_any > low_both):
+                u = jnp.where(single, rhs, u)
+            wide(c, p)[rows, columns] = rhs
+            wide(3 + c, p)[rows, columns] = sigma
+            weight(c, p)[rows, columns] = w
+            iterate(c, p)[rows, columns] = u
 
 
 def faces(u, p):
@@ -427,11 +438,15 @@
         def main(field):
             return (rhs if field < 3 else sigma)[field % 3, p - LOW]
 
-        def halo(field, side):
-            at, count = (Y_LOW, Y_HIGH)[side][p, field]
-            return (y_low, y_high)[side][at : at + count] if count else None
-
-        spread(p, main, halo, packed[p - LOW], own_edge(p, y_low, y_high), wide, weight, iterate)
+        def tile(field):
+            target = wide(field, p)
+            for ref, layout, below in ((y_low, Y_LOW, True), (y_high, Y_HIGH, False)):
+                at, count = layout[p, field]
+                start = 24 - count if below else BY
+                target[start : start + count, 0:BZ] = ref[at : at + count]
+            return target[BY:24, 0:BZ]
+
+        spread(p, main, tile, packed[p - LOW], own_edge(p, y_low, y_high), wide, weight, iterate)
 
     p = OWN[0]
     prev = f = faces(iterate, p)
@@ -473,18 +488,19 @@
     second_part, second_carry, nodal_part, nodal_carry, near = (
         plane_arrays(kind, ref) for kind, ref in list(zip(FIELDS, inner))[5:]
     )
+    upper = lax.broadcasted_iota(jnp.int32, (8, BZ), 0) < 4
     for p in OUTER["wide"]:
         ref, layout = (low, X_LOW) if p < LOW else (high, X_HIGH)
 
         def main(field):
             return ref[layout[p, field] : layout[p, field] + BY]
 
-        def halo(field, side):
-            at, count = layout[p, field, side]
-            return ref[at : at + count] if count else None
+        def tile(field):
+            (below, count), (above, _) = layout[p, field, BELOW], layout[p, field, ABOVE]
+            return jnp.where(upper, ref[above : above + 8], ref[below + count - 8 : below + count])
 
         packed, edge = layout[p, "packed"], layout[p, "edge"]
-        spread(p, main, halo, ref[packed : packed + 8], ref[edge : edge + 4], wide, weight, iterate)
+        spread(p, main, tile, ref[packed : packed + 8], ref[edge : edge + 4], wide, weight, iterate)
 
     first, last = INNER["second"][0] - 1, INNER["second"][-1]
     prev = smooth(range(1, first), faces(iterate, 0), wide, weight, iterate, second_iter)
@@ -539,6 +555,7 @@
 def on_device(rhs, conductivity, fraction, region, flags):
     f32 = functools.partial(jax.ShapeDtypeStruct, dtype=jnp.float32)
     ypar = (lax.axis_index("gy") & 1).astype(jnp.int32).reshape(1)
+    zpar = (lax.rem(lax.axis_index("gz"), 2)).astype(jnp.int32).reshape(1)
 
     block = f32((3, BX, BY, BZ))
     lane_block = f32((BX, 8, BZ))
@@ -555,14 +572,14 @@
         ),
     )(*(pltpu.with_memory_space_constraint(a, pltpu.HBM) for a in (conductivity, rhs, fraction, region, flags)))
 
-    from_low = shift(packed, "gz", 1)
-    from_high = shift(packed, "gz", -1)
+    from_even = lax.ppermute(packed, "gz", [(i, i ^ 1) for i in range(lax.axis_size("gz"))])
+    from_odd = gather(packed, "gz", pairs(lax.axis_size("gz"))[1])
 
     even_y, odd_y = pairs(lax.axis_size("gy"))
     payload = f32((Y_ROWS, BZ))
     to_first, to_second, packed = call(
-        send_y, (payload, payload, lane_block), [SMEM] + [VMEM] * 5
-    )(ypar, rhs, sigma, first_iter, from_low, from_high)
+        send_y, (payload, payload, lane_block), [SMEM] * 2 + [VMEM] * 5
+    )(ypar, zpar, rhs, sigma, first_iter, from_even, from_odd)
     first = gather(to_first, "gy", even_y)
     second = gather(to_second, "gy", odd_y)
 

time: 52.9 us -> 48.7 us (0.921)
  blocking collectives: 8.82 us -> 21.1 us
  starting transfers between devices: 26.5 us -> 14.3 us
  waiting for transfers between devices: 10.9 us -> 6.94 us
    ppermute x4 -> x2, starting transfers between devices: 26.5 us -> 9.48 us  [shift(): lax.ppermute(value, axis, [(i, (i + step) % count) for i in range(count)])]
    all_gather x2 -> x3, blocking collectives: 8.82 us -> 21.1 us  [gather(): lax.all_gather(value, axis, axis=0, tiled=False, axis_index_groups=groups)]
    ppermute x0 -> x1, starting transfers between devices: none -> 4.82 us  [on_device(): lax.ppermute(packed, 'gz', [(i, i ^ 1) for i in range(lax.axis_size('gz'))])]
    ppermute x4 -> x2, waiting for transfers between devices: 10.9 us -> 6.93 us  [shift(): lax.ppermute(value, axis, [(i, (i + step) % count) for i in range(count)])]
  transfers between devices with their start and end apart: 4 -> 3, of which waited for: 2 -> 1; matrix products, arithmetic and copies ran while one was open for 0% -> 0% of each run, Pallas kernels for 4% -> 4%
where the time goes in v6:
time: 48.7 us; the launch traced here: 48.5 us
  blocking collectives  21.1 us (43%)
  starting transfers between devices  14.3 us (29%)
  waiting for transfers between devices  6.94 us (14%)
  Pallas kernels  6.1 us (13%)
    all_gather x3, blocking collectives, gather(): lax.all_gather(value, axis, axis=0, tiled=False, axis_index_groups=groups)  21.1 us
    ppermute x2, starting transfers between devices, shift(): lax.ppermute(value, axis, [(i, (i + step) % count) for i in range(count)])  9.48 us
    ppermute x2, waiting for transfers between devices, shift(): lax.ppermute(value, axis, [(i, (i + step) % count) for i in range(count)])  6.93 us
    ppermute x1, starting transfers between devices, on_device(): lax.ppermute(packed, 'gz', [(i, i ^ 1) for i in range(lax.axis_size('gz'))])  4.82 us
    pallas_call x1, Pallas kernels, on_device(): call(stencil_outer, block, [VMEM] * (5 + len(FIELDS)), scratch=[pltpu.VME...  2.48 us
    pallas_call x1, Pallas kernels, on_device(): call(stencil_inner, (f32((3, BY, BZ)), *(f32((FIELDS[kind], len(INNER[kin...  1.96 us
    pallas_call x1, Pallas kernels, on_device(): call(prepare, (block, block, block, lane_block), [HBM] * 5, scratch=(pltp...  1.37 us
  transfers between devices with their start and end apart: 3, of which 1 were waited for; matrix products, arithmetic and copies ran while one was open for 0% of the time, Pallas kernels for 4%

profile of v6, /device:TPU:1, one launch (start us, length us, event | category | flops | bytes accessed | tf_op | source)
XLA Modules:
  0.0 48.5 jit_solution(9976541992699310279)
XLA Ops:
  0.0 1.4 %shard_map.55 = (f32[3,8,16,128]{3,2,1,0:T(8,128)S(1)}, f32[3,8,16,128]{3,2,1,0:T(8,128)S(1)}, f32[3,8,16,128]{3,2,1,0:T(8,128)S(1)}, f32[8,8,128]{2,1,0:T(8,128)S(1)}) custom-call(f32[8]{0:T(128)} %cond_in.1, f32[3,8,16,128]{3,2,1,0:T(8,128)} %rhs_in.1, f32[3,8,16,128]{3,2,1,0:T(8,128)} %fraction_in.1, s32[8,16,128]{2,1,0:T(8,128)} %region_in.1, ...), custom_call_target="tpu_custom_call" | custom-call | flops 1000000 | bytes 1000000 | tf_op jit(solution)/shard_map/pallas_call | solution.py:562
  1.4 4.8 %collective-permute-start = (f32[8,8,128]{2,1,0:T(8,128)S(1)}, f32[8,8,128]{2,1,0:T(8,128)S(1)}, u32[]{:S(2)}, u32[]{:S(2)}) collective-permute-start(f32[8,8,128]{2,1,0:T(8,128)S(1)} %get-tuple-element.30), channel_id=1, source_target_pairs={{0,1},{1,0},{2,3},{3,2},{4,5},{5,4},{6,7},{7,6},{8,9},{9,8},{10,11... | collective-permute-start | bytes 98312 | tf_op jit(solution)/shard_map/ppermute | solution.py:575
  6.2 12.5 %all-gather = f32[16,8,128]{2,1,0:T(8,128)S(1)} all-gather(f32[8,8,128]{2,1,0:T(8,128)S(1)} %get-tuple-element.30), channel_id=2, replica_groups={{1,2},{3,4},{5,6},{7,8},{9,10},{11,0},{13,14},{15,16},{17,18},{19,20},{..., dimensions={0}, use_global_device_ids=true | all-gather | bytes 98304 | tf_op jit(solution)/shard_map/all_gather | solution.py:547
  18.8 0.0 collective-permute-done.from_even
  18.8 0.1 shard_map.56
  18.8 3.4 %all-gather.1 = f32[336,128]{1,0:T(8,128)S(1)} all-gather(f32[168,128]{1,0:T(8,128)S(1)} %get-tuple-element.32), channel_id=3, replica_groups={{0,12},{24,36},{1,13},{25,37},{2,14},{26,38},{3,15},{27,39},{4,16},{28,..., dimensions={0}, use_global_device_ids=true | all-gather | bytes 258048 | tf_op jit(solution)/shard_map/all_gather | solution.py:547
  22.2 5.1 %all-gather.2 = f32[336,128]{1,0:T(8,128)S(1)} all-gather(f32[168,128]{1,0:T(8,128)S(1)} %get-tuple-element.33), channel_id=4, replica_groups={{12,24},{36,0},{13,25},{37,1},{14,26},{38,2},{15,27},{39,3},{16,28},{40..., dimensions={0}, use_global_device_ids=true | all-gather | bytes 258048 | tf_op jit(solution)/shard_map/all_gather | solution.py:547
  27.4 0.2 shard_map.57
  27.6 7.6 %collective-permute-start.2 = (f32[416,128]{1,0:T(8,128)S(1)}, f32[416,128]{1,0:T(8,128)S(1)}, u32[]{:S(2)}, u32[]{:S(2)}) collective-permute-start(f32[416,128]{1,0:T(8,128)S(1)} %get-tuple-element.35), channel_id=1, source_target_pairs={{0,720},{48,0},{96,48},{144,96},{192,144},{240,192},{288,240},{336... | collective-permute-start | bytes 638984 | tf_op jit(solution)/shard_map/ppermute | solution.py:552
  35.2 1.9 %collective-permute-start.1 = (f32[336,128]{1,0:T(8,128)S(1)}, f32[336,128]{1,0:T(8,128)S(1)}, u32[]{:S(2)}, u32[]{:S(2)}) collective-permute-start(f32[336,128]{1,0:T(8,128)S(1)} %get-tuple-element.34), channel_id=1, source_target_pairs={{0,48},{48,96},{96,144},{144,192},{192,240},{240,288},{288,336},{3... | collective-permute-start | bytes 516104 | tf_op jit(solution)/shard_map/ppermute | solution.py:552
  37.1 2.0 %shard_map.58 = (f32[3,16,128]{2,1,0:T(8,128)S(1)}, f32[6,8,24,256]{3,2,1,0:T(8,128)S(1)}, f32[3,8,24,256]{3,2,1,0:T(8,128)S(1)}, f32[3,8,24,256]{3,2,1,0:T(8,12...) custom-call(f32[3,8,16,128]{3,2,1,0:T(8,128)S(1)} %get-tuple-element, ...), custom_call_target="tpu_custom_call" | custom-call | flops 20000000 | bytes 1000000 | tf_op jit(solution)/shard_map/pallas_call | solution.py:592
  39.1 6.9 %collective-permute-done.1.low = f32[336,128]{1,0:T(8,128)S(1)} collective-permute-done((f32[336,128]{1,0:T(8,128)S(1)}, f32[336,128]{1,0:T(8,128)S(1)}, u32[]{:S(2)}, u32[]{:S(2)}) %collective-permute-start.1) | collective-permute-done | bytes 172064 | tf_op jit(solution)/shard_map/ppermute | solution.py:552
  46.0 0.0 collective-permute-done.2.high
  46.0 2.5 %shard_map.59 = f32[3,8,16,128]{3,2,1,0:T(8,128)} custom-call(f32[3,8,16,128]{3,2,1,0:T(8,128)S(1)} %get-tuple-element.27.rhs, f32[3,8,16,128]{3,2,1,0:T(8,128)S(1)} %get-tuple-element.28.sigma, f32[336,128]{1,0:T(8,128)S(1)} %collective-permute-done.1.low, f32[416,128]{1,0:T(8,128)S(1)} %collective-permute-done.2.high, ...), custom_call_target="tpu_custom_call" | custom-call | flops 1000000 | bytes 1000000 | tf_op jit(solution)/shard_map/pallas_call | solution.py:598
Async XLA Ops:
  1.4 17.4 %collective-permute-start = (f32[8,8,128]{2,1,0:T(8,128)S(1)}, f32[8,8,128]{2,1,0:T(8,128)S(1)}, u32[]{:S(2)}, u32[]{:S(2)}) collective-permute-start(f32[8,8,128]{2,1,0:T(8,128)S(1)} %get-tuple-element.30), channel_id=1, source_target_pairs={{0,1},{1,0},{2,3},{3,2},{4,5},{5,4},{6,7},{7,6},{8,9},{9,8},{10,11... | collective-permute-start | bytes 98312 | tf_op jit(solution)/shard_map/ppermute | solution.py:575
  27.6 18.4 %collective-permute-start.2 = (f32[416,128]{1,0:T(8,128)S(1)}, f32[416,128]{1,0:T(8,128)S(1)}, u32[]{:S(2)}, u32[]{:S(2)}) collective-permute-start(f32[416,128]{1,0:T(8,128)S(1)} %get-tuple-element.35), channel_id=1, source_target_pairs={{0,720},{48,0},{96,48},{144,96},{192,144},{240,192},{288,240},{336... | collective-permute-start | bytes 638984 | tf_op jit(solution)/shard_map/ppermute | solution.py:552
  35.2 10.8 %collective-permute-start.1 = (f32[336,128]{1,0:T(8,128)S(1)}, f32[336,128]{1,0:T(8,128)S(1)}, u32[]{:S(2)}, u32[]{:S(2)}) collective-permute-start(f32[336,128]{1,0:T(8,128)S(1)} %get-tuple-element.34), channel_id=1, source_target_pairs={{0,48},{48,96},{96,144},{144,192},{192,240},{240,288},{288,336},{3... | collective-permute-start | bytes 516104 | tf_op jit(solution)/shard_map/ppermute | solution.py:552

commit v7 on v6

--- a/solution.py
+++ b/solution.py
@@ -179,12 +179,14 @@
         packed_out[x] = packed
 
 
-def send_y(ypar, zpar, rhs, sigma, first_iter, from_even, from_odd, first_out, second_out, packed):
+def send_y(
+    ypar, zpar, zlast, rhs, sigma, first_iter, from_even, from_odd, from_last, first_out, second_out, packed
+):
     below = (lanes((8, BZ)) % 8) < LOW
     odd = (lanes((4, BZ)) // 8) % 2
     below = below == (zpar[0] == 0)
     for x in range(BX):
-        packed[x] = jnp.where(below, jnp.where(zpar[0] == 0, from_odd[0, x], from_odd[1, x]), from_even[x])
+        packed[x] = jnp.where(below, jnp.where(zpar[0] == 0, from_odd[0, x], from_odd[1, x]), jnp.where(zlast[0] == 0, from_even[x], from_last[x]))
 
     def fill(out, layout, side):
         for p in OWN:
@@ -555,6 +557,7 @@
 def on_device(rhs, conductivity, fraction, region, flags):
     f32 = functools.partial(jax.ShapeDtypeStruct, dtype=jnp.float32)
     ypar = (lax.axis_index("gy") & 1).astype(jnp.int32).reshape(1)
+    zlast = (lax.axis_index("gz") >= lax.axis_size("gz") - 2).astype(jnp.int32).reshape(1)
     zpar = (lax.rem(lax.axis_index("gz"), 2)).astype(jnp.int32).reshape(1)
 
     block = f32((3, BX, BY, BZ))
@@ -572,14 +575,16 @@
         ),
     )(*(pltpu.with_memory_space_constraint(a, pltpu.HBM) for a in (conductivity, rhs, fraction, region, flags)))
 
-    from_even = lax.ppermute(packed, "gz", [(i, i ^ 1) for i in range(lax.axis_size("gz"))])
-    from_odd = gather(packed, "gz", pairs(lax.axis_size("gz"))[1])
+    nz = lax.axis_size("gz")
+    from_even = lax.ppermute(packed, "gz", [(i, i ^ 1) for i in range(nz - 2)])
+    from_odd = gather(packed, "gz", pairs(nz)[1])
+    from_last = lax.ppermute(packed, "gz", [(nz - 2, nz - 1), (nz - 1, nz - 2)])
 
     even_y, odd_y = pairs(lax.axis_size("gy"))
     payload = f32((Y_ROWS, BZ))
     to_first, to_second, packed = call(
-        send_y, (payload, payload, lane_block), [SMEM] * 2 + [VMEM] * 5
-    )(ypar, zpar, rhs, sigma, first_iter, from_even, from_odd)
+        send_y, (payload, payload, lane_block), [SMEM] * 3 + [VMEM] * 6
+    )(ypar, zpar, zlast, rhs, sigma, first_iter, from_even, from_odd, from_last)
     first = gather(to_first, "gy", even_y)
     second = gather(to_second, "gy", odd_y)
 

time: 48.7 us -> 49.4 us (1.014)
  starting transfers between devices: 14.3 us -> 15 us
    ppermute x1 -> x2, starting transfers between devices: 4.82 us -> 5.48 us  [the longest x1 4.82 us: on_device(): from_even = lax.ppermute(packed, 'gz', [(i, i ^ 1) for i in range(nz - 2)])]
  transfers between devices with their start and end apart: 3 -> 4, of which waited for: 1 -> 1; matrix products, arithmetic and copies ran while one was open for 0% -> 0% of each run, Pallas kernels for 4% -> 4%
where the time goes in v7:
time: 49.4 us; the launch traced here: 49.2 us
  blocking collectives  21.1 us (43%)
  starting transfers between devices  15 us (30%)
  waiting for transfers between devices  6.94 us (14%)
  Pallas kernels  6.11 us (12%)
    all_gather x3, blocking collectives, gather(): lax.all_gather(value, axis, axis=0, tiled=False, axis_index_groups=groups)  21.1 us
    ppermute x2, starting transfers between devices, shift(): lax.ppermute(value, axis, [(i, (i + step) % count) for i in range(count)])  9.48 us
    ppermute x2, waiting for transfers between devices, shift(): lax.ppermute(value, axis, [(i, (i + step) % count) for i in range(count)])  6.93 us
    ppermute x1, starting transfers between devices, on_device(): from_even = lax.ppermute(packed, 'gz', [(i, i ^ 1) for i in range(nz - 2)])  4.82 us
    pallas_call x1, Pallas kernels, on_device(): call(stencil_outer, block, [VMEM] * (5 + len(FIELDS)), scratch=[pltpu.VME...  2.48 us
    pallas_call x1, Pallas kernels, on_device(): call(stencil_inner, (f32((3, BY, BZ)), *(f32((FIELDS[kind], len(INNER[kin...  1.96 us
    pallas_call x1, Pallas kernels, on_device(): call(prepare, (block, block, block, lane_block), [HBM] * 5, scratch=(pltp...  1.37 us
  transfers between devices with their start and end apart: 4, of which 1 were waited for; matrix products, arithmetic and copies ran while one was open for 0% of the time, Pallas kernels for 4%

profile of v7, /device:TPU:1, one launch (start us, length us, event | category | flops | bytes accessed | tf_op | source)
XLA Modules:
  0.0 49.2 jit_solution(1345086765332319914)
XLA Ops:
  0.0 1.4 %shard_map.55 = (f32[3,8,16,128]{3,2,1,0:T(8,128)S(1)}, f32[3,8,16,128]{3,2,1,0:T(8,128)S(1)}, f32[3,8,16,128]{3,2,1,0:T(8,128)S(1)}, f32[8,8,128]{2,1,0:T(8,128)S(1)}) custom-call(f32[8]{0:T(128)} %cond_in.1, f32[3,8,16,128]{3,2,1,0:T(8,128)} %rhs_in.1, f32[3,8,16,128]{3,2,1,0:T(8,128)} %fraction_in.1, s32[8,16,128]{2,1,0:T(8,128)} %region_in.1, ...), custom_call_target="tpu_custom_call" | custom-call | flops 1000000 | bytes 1000000 | tf_op jit(solution)/shard_map/pallas_call | solution.py:565
  1.4 0.7 %collective-permute-start.1 = (f32[8,8,128]{2,1,0:T(8,128)S(1)}, f32[8,8,128]{2,1,0:T(8,128)S(1)}, u32[]{:S(2)}, u32[]{:S(2)}) collective-permute-start(f32[8,8,128]{2,1,0:T(8,128)S(1)} %get-tuple-element.30), channel_id=1, source_target_pairs={{10,11},{11,10},{22,23},{23,22},{34,35},{35,34},{46,47},{47,46},{5... | collective-permute-start | bytes 98312 | tf_op jit(solution)/shard_map/ppermute | solution.py:581
  2.0 4.8 %collective-permute-start = (f32[8,8,128]{2,1,0:T(8,128)S(1)}, f32[8,8,128]{2,1,0:T(8,128)S(1)}, u32[]{:S(2)}, u32[]{:S(2)}) collective-permute-start(f32[8,8,128]{2,1,0:T(8,128)S(1)} %get-tuple-element.30), channel_id=1, source_target_pairs={{0,1},{1,0},{2,3},{3,2},{4,5},{5,4},{6,7},{7,6},{8,9},{9,8},{12,13... | collective-permute-start | bytes 98312 | tf_op jit(solution)/shard_map/ppermute | solution.py:579
  6.9 12.5 %all-gather = f32[16,8,128]{2,1,0:T(8,128)S(1)} all-gather(f32[8,8,128]{2,1,0:T(8,128)S(1)} %get-tuple-element.30), channel_id=2, replica_groups={{1,2},{3,4},{5,6},{7,8},{9,10},{11,0},{13,14},{15,16},{17,18},{19,20},{..., dimensions={0}, use_global_device_ids=true | all-gather | bytes 98304 | tf_op jit(solution)/shard_map/all_gather | solution.py:549
  19.4 0.0 collective-permute-done.1.from_last
  19.4 0.0 collective-permute-done.from_even
  19.4 0.1 shard_map.56
  19.5 3.4 %all-gather.1 = f32[336,128]{1,0:T(8,128)S(1)} all-gather(f32[168,128]{1,0:T(8,128)S(1)} %get-tuple-element.32), channel_id=3, replica_groups={{0,12},{24,36},{1,13},{25,37},{2,14},{26,38},{3,15},{27,39},{4,16},{28,..., dimensions={0}, use_global_device_ids=true | all-gather | bytes 258048 | tf_op jit(solution)/shard_map/all_gather | solution.py:549
  22.9 5.1 %all-gather.2 = f32[336,128]{1,0:T(8,128)S(1)} all-gather(f32[168,128]{1,0:T(8,128)S(1)} %get-tuple-element.33), channel_id=4, replica_groups={{12,24},{36,0},{13,25},{37,1},{14,26},{38,2},{15,27},{39,3},{16,28},{40..., dimensions={0}, use_global_device_ids=true | all-gather | bytes 258048 | tf_op jit(solution)/shard_map/all_gather | solution.py:549
  28.1 0.2 shard_map.57
  28.3 7.6 %collective-permute-start.3 = (f32[416,128]{1,0:T(8,128)S(1)}, f32[416,128]{1,0:T(8,128)S(1)}, u32[]{:S(2)}, u32[]{:S(2)}) collective-permute-start(f32[416,128]{1,0:T(8,128)S(1)} %get-tuple-element.35), channel_id=1, source_target_pairs={{0,720},{48,0},{96,48},{144,96},{192,144},{240,192},{288,240},{336... | collective-permute-start | bytes 638984 | tf_op jit(solution)/shard_map/ppermute | solution.py:554
  35.9 1.9 %collective-permute-start.2 = (f32[336,128]{1,0:T(8,128)S(1)}, f32[336,128]{1,0:T(8,128)S(1)}, u32[]{:S(2)}, u32[]{:S(2)}) collective-permute-start(f32[336,128]{1,0:T(8,128)S(1)} %get-tuple-element.34), channel_id=1, source_target_pairs={{0,48},{48,96},{96,144},{144,192},{192,240},{240,288},{288,336},{3... | collective-permute-start | bytes 516104 | tf_op jit(solution)/shard_map/ppermute | solution.py:554
  37.8 2.0 %shard_map.58 = (f32[3,16,128]{2,1,0:T(8,128)S(1)}, f32[6,8,24,256]{3,2,1,0:T(8,128)S(1)}, f32[3,8,24,256]{3,2,1,0:T(8,128)S(1)}, f32[3,8,24,256]{3,2,1,0:T(8,12...) custom-call(f32[3,8,16,128]{3,2,1,0:T(8,128)S(1)} %get-tuple-element, ...), custom_call_target="tpu_custom_call" | custom-call | flops 20000000 | bytes 1000000 | tf_op jit(solution)/shard_map/pallas_call | solution.py:597
  39.7 6.9 %collective-permute-done.2.low = f32[336,128]{1,0:T(8,128)S(1)} collective-permute-done((f32[336,128]{1,0:T(8,128)S(1)}, f32[336,128]{1,0:T(8,128)S(1)}, u32[]{:S(2)}, u32[]{:S(2)}) %collective-permute-start.2) | collective-permute-done | bytes 172064 | tf_op jit(solution)/shard_map/ppermute | solution.py:554
  46.7 0.0 collective-permute-done.3.high
  46.7 2.5 %shard_map.59 = f32[3,8,16,128]{3,2,1,0:T(8,128)} custom-call(f32[3,8,16,128]{3,2,1,0:T(8,128)S(1)} %get-tuple-element.27.rhs, f32[3,8,16,128]{3,2,1,0:T(8,128)S(1)} %get-tuple-element.28.sigma, f32[336,128]{1,0:T(8,128)S(1)} %collective-permute-done.2.low, f32[416,128]{1,0:T(8,128)S(1)} %collective-permute-done.3.high, ...), custom_call_target="tpu_custom_call" | custom-call | flops 1000000 | bytes 1000000 | tf_op jit(solution)/shard_map/pallas_call | solution.py:603
Async XLA Ops:
  1.4 18.1 %collective-permute-start.1 = (f32[8,8,128]{2,1,0:T(8,128)S(1)}, f32[8,8,128]{2,1,0:T(8,128)S(1)}, u32[]{:S(2)}, u32[]{:S(2)}) collective-permute-start(f32[8,8,128]{2,1,0:T(8,128)S(1)} %get-tuple-element.30), channel_id=1, source_target_pairs={{10,11},{11,10},{22,23},{23,22},{34,35},{35,34},{46,47},{47,46},{5... | collective-permute-start | bytes 98312 | tf_op jit(solution)/shard_map/ppermute | solution.py:581
  2.0 17.4 %collective-permute-start = (f32[8,8,128]{2,1,0:T(8,128)S(1)}, f32[8,8,128]{2,1,0:T(8,128)S(1)}, u32[]{:S(2)}, u32[]{:S(2)}) collective-permute-start(f32[8,8,128]{2,1,0:T(8,128)S(1)} %get-tuple-element.30), channel_id=1, source_target_pairs={{0,1},{1,0},{2,3},{3,2},{4,5},{5,4},{6,7},{7,6},{8,9},{9,8},{12,13... | collective-permute-start | bytes 98312 | tf_op jit(solution)/shard_map/ppermute | solution.py:579
  28.3 18.4 %collective-permute-start.3 = (f32[416,128]{1,0:T(8,128)S(1)}, f32[416,128]{1,0:T(8,128)S(1)}, u32[]{:S(2)}, u32[]{:S(2)}) collective-permute-start(f32[416,128]{1,0:T(8,128)S(1)} %get-tuple-element.35), channel_id=1, source_target_pairs={{0,720},{48,0},{96,48},{144,96},{192,144},{240,192},{288,240},{336... | collective-permute-start | bytes 638984 | tf_op jit(solution)/shard_map/ppermute | solution.py:554
  35.9 10.8 %collective-permute-start.2 = (f32[336,128]{1,0:T(8,128)S(1)}, f32[336,128]{1,0:T(8,128)S(1)}, u32[]{:S(2)}, u32[]{:S(2)}) collective-permute-start(f32[336,128]{1,0:T(8,128)S(1)} %get-tuple-element.34), channel_id=1, source_target_pairs={{0,48},{48,96},{96,144},{144,192},{192,240},{240,288},{288,336},{3... | collective-permute-start | bytes 516104 | tf_op jit(solution)/shard_map/ppermute | solution.py:554

commit v8 on v7

--- a/solution.py
+++ b/solution.py
@@ -147,18 +147,20 @@
 
 
 def prepare(cond_in, rhs_in, fraction_in, region_in, flags_in, rhs, sigma, first_iter, packed_out, cond, fraction, region, flags, sems):
-    copies = [
-        pltpu.make_async_copy(source, target, sems.at[i])
-        for i, (source, target) in enumerate(
-            ((cond_in, cond), (region_in, region), (fraction_in, fraction), (flags_in, flags), (rhs_in, rhs))
-        )
-    ]
-    for copy in copies:
+    half = BX // 2
+    copies = [[pltpu.make_async_copy(cond_in, cond, sems.at[0])], []]
+    for i in range(2):
+        part = pl.ds(i * half, half)
+        copies[i].append(pltpu.make_async_copy(region_in.at[part], region.at[part], sems.at[1 + 4 * i]))
+        for j, (source, target) in enumerate(((fraction_in, fraction), (flags_in, flags), (rhs_in, rhs))):
+            copies[i].append(pltpu.make_async_copy(source.at[:, part], target.at[:, part], sems.at[2 + 4 * i + j]))
+    for copy in copies[0] + copies[1]:
         copy.start()
-    for copy in copies:
-        copy.wait()
     group = lanes((8, BZ)) // 8
     for x in range(BX):
+        if x % half == 0:
+            for copy in copies[x // half]:
+                copy.wait()
         where = region[x]
         conductivity = jnp.full((BY, BZ), cond[0], jnp.float32)
         for number in range(1, 8):
@@ -571,7 +573,7 @@
             pltpu.VMEM((3, BX, BY, BZ), jnp.float32),
             pltpu.VMEM((BX, BY, BZ), jnp.int32),
             pltpu.VMEM((3, BX, BY, BZ), jnp.int32),
-            pltpu.SemaphoreType.DMA((5,)),
+            pltpu.SemaphoreType.DMA((9,)),
         ),
     )(*(pltpu.with_memory_space_constraint(a, pltpu.HBM) for a in (conductivity, rhs, fraction, region, flags)))
 

time: 49.4 us -> 49.4 us (level)
  no operation moved by 1% of the time
where the time goes in v8:
time: 49.4 us; the launch traced here: 49.2 us
  blocking collectives  21.1 us (43%)
  starting transfers between devices  15 us (30%)
  waiting for transfers between devices  6.94 us (14%)
  Pallas kernels  6.1 us (12%)
    all_gather x3, blocking collectives, gather(): lax.all_gather(value, axis, axis=0, tiled=False, axis_index_groups=groups)  21.1 us
    ppermute x2, starting transfers between devices, shift(): lax.ppermute(value, axis, [(i, (i + step) % count) for i in range(count)])  9.48 us
    ppermute x2, waiting for transfers between devices, shift(): lax.ppermute(value, axis, [(i, (i + step) % count) for i in range(count)])  6.93 us
    ppermute x1, starting transfers between devices, on_device(): from_even = lax.ppermute(packed, 'gz', [(i, i ^ 1) for i in range(nz - 2)])  4.82 us
    pallas_call x1, Pallas kernels, on_device(): call(stencil_outer, block, [VMEM] * (5 + len(FIELDS)), scratch=[pltpu.VME...  2.48 us
    pallas_call x1, Pallas kernels, on_device(): call(stencil_inner, (f32((3, BY, BZ)), *(f32((FIELDS[kind], len(INNER[kin...  1.96 us
    pallas_call x1, Pallas kernels, on_device(): call(prepare, (block, block, block, lane_block), [HBM] * 5, scratch=(pltp...  1.36 us
  transfers between devices with their start and end apart: 4, of which 1 were waited for; matrix products, arithmetic and copies ran while one was open for 0% of the time, Pallas kernels for 4%

profile of v8, /device:TPU:1, one launch (start us, length us, event | category | flops | bytes accessed | tf_op | source)
XLA Modules:
  0.0 49.2 jit_solution(11363292852505370198)
XLA Ops:
  0.0 1.4 %shard_map.55 = (f32[3,8,16,128]{3,2,1,0:T(8,128)S(1)}, f32[3,8,16,128]{3,2,1,0:T(8,128)S(1)}, f32[3,8,16,128]{3,2,1,0:T(8,128)S(1)}, f32[8,8,128]{2,1,0:T(8,128)S(1)}) custom-call(f32[8]{0:T(128)} %cond_in.1, f32[3,8,16,128]{3,2,1,0:T(8,128)} %rhs_in.1, f32[3,8,16,128]{3,2,1,0:T(8,128)} %fraction_in.1, s32[8,16,128]{2,1,0:T(8,128)} %region_in.1, ...), custom_call_target="tpu_custom_call" | custom-call | flops 1000000 | bytes 1000000 | tf_op jit(solution)/shard_map/pallas_call | solution.py:567
  1.4 0.7 %collective-permute-start.1 = (f32[8,8,128]{2,1,0:T(8,128)S(1)}, f32[8,8,128]{2,1,0:T(8,128)S(1)}, u32[]{:S(2)}, u32[]{:S(2)}) collective-permute-start(f32[8,8,128]{2,1,0:T(8,128)S(1)} %get-tuple-element.30), channel_id=1, source_target_pairs={{10,11},{11,10},{22,23},{23,22},{34,35},{35,34},{46,47},{47,46},{5... | collective-permute-start | bytes 98312 | tf_op jit(solution)/shard_map/ppermute | solution.py:583
  2.0 4.8 %collective-permute-start = (f32[8,8,128]{2,1,0:T(8,128)S(1)}, f32[8,8,128]{2,1,0:T(8,128)S(1)}, u32[]{:S(2)}, u32[]{:S(2)}) collective-permute-start(f32[8,8,128]{2,1,0:T(8,128)S(1)} %get-tuple-element.30), channel_id=1, source_target_pairs={{0,1},{1,0},{2,3},{3,2},{4,5},{5,4},{6,7},{7,6},{8,9},{9,8},{12,13... | collective-permute-start | bytes 98312 | tf_op jit(solution)/shard_map/ppermute | solution.py:581
  6.9 12.5 %all-gather = f32[16,8,128]{2,1,0:T(8,128)S(1)} all-gather(f32[8,8,128]{2,1,0:T(8,128)S(1)} %get-tuple-element.30), channel_id=2, replica_groups={{1,2},{3,4},{5,6},{7,8},{9,10},{11,0},{13,14},{15,16},{17,18},{19,20},{..., dimensions={0}, use_global_device_ids=true | all-gather | bytes 98304 | tf_op jit(solution)/shard_map/all_gather | solution.py:551
  19.4 0.0 collective-permute-done.1.from_last
  19.4 0.0 collective-permute-done.from_even
  19.4 0.1 shard_map.56
  19.5 3.4 %all-gather.1 = f32[336,128]{1,0:T(8,128)S(1)} all-gather(f32[168,128]{1,0:T(8,128)S(1)} %get-tuple-element.32), channel_id=3, replica_groups={{0,12},{24,36},{1,13},{25,37},{2,14},{26,38},{3,15},{27,39},{4,16},{28,..., dimensions={0}, use_global_device_ids=true | all-gather | bytes 258048 | tf_op jit(solution)/shard_map/all_gather | solution.py:551
  22.9 5.1 %all-gather.2 = f32[336,128]{1,0:T(8,128)S(1)} all-gather(f32[168,128]{1,0:T(8,128)S(1)} %get-tuple-element.33), channel_id=4, replica_groups={{12,24},{36,0},{13,25},{37,1},{14,26},{38,2},{15,27},{39,3},{16,28},{40..., dimensions={0}, use_global_device_ids=true | all-gather | bytes 258048 | tf_op jit(solution)/shard_map/all_gather | solution.py:551
  28.1 0.2 shard_map.57
  28.3 7.6 %collective-permute-start.3 = (f32[416,128]{1,0:T(8,128)S(1)}, f32[416,128]{1,0:T(8,128)S(1)}, u32[]{:S(2)}, u32[]{:S(2)}) collective-permute-start(f32[416,128]{1,0:T(8,128)S(1)} %get-tuple-element.35), channel_id=1, source_target_pairs={{0,720},{48,0},{96,48},{144,96},{192,144},{240,192},{288,240},{336... | collective-permute-start | bytes 638984 | tf_op jit(solution)/shard_map/ppermute | solution.py:556
  35.8 1.9 %collective-permute-start.2 = (f32[336,128]{1,0:T(8,128)S(1)}, f32[336,128]{1,0:T(8,128)S(1)}, u32[]{:S(2)}, u32[]{:S(2)}) collective-permute-start(f32[336,128]{1,0:T(8,128)S(1)} %get-tuple-element.34), channel_id=1, source_target_pairs={{0,48},{48,96},{96,144},{144,192},{192,240},{240,288},{288,336},{3... | collective-permute-start | bytes 516104 | tf_op jit(solution)/shard_map/ppermute | solution.py:556
  37.8 2.0 %shard_map.58 = (f32[3,16,128]{2,1,0:T(8,128)S(1)}, f32[6,8,24,256]{3,2,1,0:T(8,128)S(1)}, f32[3,8,24,256]{3,2,1,0:T(8,128)S(1)}, f32[3,8,24,256]{3,2,1,0:T(8,12...) custom-call(f32[3,8,16,128]{3,2,1,0:T(8,128)S(1)} %get-tuple-element, ...), custom_call_target="tpu_custom_call" | custom-call | flops 20000000 | bytes 1000000 | tf_op jit(solution)/shard_map/pallas_call | solution.py:599
  39.7 6.9 %collective-permute-done.2.low = f32[336,128]{1,0:T(8,128)S(1)} collective-permute-done((f32[336,128]{1,0:T(8,128)S(1)}, f32[336,128]{1,0:T(8,128)S(1)}, u32[]{:S(2)}, u32[]{:S(2)}) %collective-permute-start.2) | collective-permute-done | bytes 172064 | tf_op jit(solution)/shard_map/ppermute | solution.py:556
  46.7 0.0 collective-permute-done.3.high
  46.7 2.5 %shard_map.59 = f32[3,8,16,128]{3,2,1,0:T(8,128)} custom-call(f32[3,8,16,128]{3,2,1,0:T(8,128)S(1)} %get-tuple-element.27.rhs, f32[3,8,16,128]{3,2,1,0:T(8,128)S(1)} %get-tuple-element.28.sigma, f32[336,128]{1,0:T(8,128)S(1)} %collective-permute-done.2.low, f32[416,128]{1,0:T(8,128)S(1)} %collective-permute-done.3.high, ...), custom_call_target="tpu_custom_call" | custom-call | flops 1000000 | bytes 1000000 | tf_op jit(solution)/shard_map/pallas_call | solution.py:605
Async XLA Ops:
  1.4 18.1 %collective-permute-start.1 = (f32[8,8,128]{2,1,0:T(8,128)S(1)}, f32[8,8,128]{2,1,0:T(8,128)S(1)}, u32[]{:S(2)}, u32[]{:S(2)}) collective-permute-start(f32[8,8,128]{2,1,0:T(8,128)S(1)} %get-tuple-element.30), channel_id=1, source_target_pairs={{10,11},{11,10},{22,23},{23,22},{34,35},{35,34},{46,47},{47,46},{5... | collective-permute-start | bytes 98312 | tf_op jit(solution)/shard_map/ppermute | solution.py:583
  2.0 17.4 %collective-permute-start = (f32[8,8,128]{2,1,0:T(8,128)S(1)}, f32[8,8,128]{2,1,0:T(8,128)S(1)}, u32[]{:S(2)}, u32[]{:S(2)}) collective-permute-start(f32[8,8,128]{2,1,0:T(8,128)S(1)} %get-tuple-element.30), channel_id=1, source_target_pairs={{0,1},{1,0},{2,3},{3,2},{4,5},{5,4},{6,7},{7,6},{8,9},{9,8},{12,13... | collective-permute-start | bytes 98312 | tf_op jit(solution)/shard_map/ppermute | solution.py:581
  28.3 18.4 %collective-permute-start.3 = (f32[416,128]{1,0:T(8,128)S(1)}, f32[416,128]{1,0:T(8,128)S(1)}, u32[]{:S(2)}, u32[]{:S(2)}) collective-permute-start(f32[416,128]{1,0:T(8,128)S(1)} %get-tuple-element.35), channel_id=1, source_target_pairs={{0,720},{48,0},{96,48},{144,96},{192,144},{240,192},{288,240},{336... | collective-permute-start | bytes 638984 | tf_op jit(solution)/shard_map/ppermute | solution.py:556
  35.8 10.8 %collective-permute-start.2 = (f32[336,128]{1,0:T(8,128)S(1)}, f32[336,128]{1,0:T(8,128)S(1)}, u32[]{:S(2)}, u32[]{:S(2)}) collective-permute-start(f32[336,128]{1,0:T(8,128)S(1)} %get-tuple-element.34), channel_id=1, source_target_pairs={{0,48},{48,96},{96,144},{144,192},{192,240},{240,288},{288,336},{3... | collective-permute-start | bytes 516104 | tf_op jit(solution)/shard_map/ppermute | solution.py:556
